TPU v7x, 32 devices: a whole 2x2x4 slice. The times are simulated.
32 devices in a mesh: dp: 16 (over z, y, x), tensor: 2 (over core).
Axes of the slice: x: 2, y: 2, z: 4, core: 2. Of those that a mesh axis runs over, the one named last changes fastest.
Arguments:
- tokens: bfloat16 [25088, 1024], P('dp'), may hold values from -6 to 6
- attention_gain: float32 [1024], replicated, may hold values from 0.25 to 1.75
- attention_shift: float32 [1024], replicated, may hold values from -3 to 3
- input_weight: bfloat16 [1024, 3, 1024], P(None, None, 'tensor'), may hold values from -0.1875 to 0.1875
- query_bias: float32 [1024], P('tensor'), may hold values from -3 to 3
- value_bias: float32 [1024], P('tensor'), may hold values from -3 to 3
- output_weight: bfloat16 [1024, 1024], P('tensor'), may hold values from -1.5 to 1.5
- output_bias: float32 [1024], replicated, may hold values from -3 to 3
- feedforward_gain: float32 [1024], replicated, may hold values from 0.25 to 1.75
- feedforward_shift: float32 [1024], replicated, may hold values from -3 to 3
- expand_weight: bfloat16 [1024, 4096], P(None, 'tensor'), may hold values from -0.1875 to 0.1875
- expand_bias: float32 [4096], P('tensor'), may hold values from -3 to 3
- reduce_weight: bfloat16 [4096, 1024], P('tensor'), may hold values from -0.09375 to 0.09375
- reduce_bias: float32 [1024], replicated, may hold values from -3 to 3
- cotangent: bfloat16 [25088, 1024], P('dp'), may hold values from -6 to 6
Outputs:
- block_out: bfloat16 [25088, 1024], P('dp')
- tokens_gradient: bfloat16 [25088, 1024], P('dp')
- attention_gain_gradient: float32 [1024], replicated
- attention_shift_gradient: float32 [1024], replicated
- input_weight_gradient: float32 [1024, 3, 1024], P(None, None, 'tensor')
- query_bias_gradient: float32 [1024], P('tensor')
- value_bias_gradient: float32 [1024], P('tensor')
- output_weight_gradient: float32 [1024, 1024], P('tensor')
- output_bias_gradient: float32 [1024], replicated
- feedforward_gain_gradient: float32 [1024], replicated
- feedforward_shift_gradient: float32 [1024], replicated
- expand_weight_gradient: float32 [1024, 4096], P(None, 'tensor')
- expand_bias_gradient: float32 [4096], P('tensor')
- reduce_weight_gradient: float32 [4096, 1024], P('tensor')
- reduce_bias_gradient: float32 [1024], replicated
All inputs are finite; a program needn't handle non-finite values.
Results may differ from a plain program's by a relative error of at most 0.013.
The roundings to bfloat16 on the way count: a program that leaves them out, or rounds other values in their place, can miss the bound.
Values may be sent and summed in bfloat16 or wider, within the bound.
A program may use at most 384 MiB of HBM per device.

v0:
```python
import jax
import jax.numpy as jnp
from jax import lax
from jax.sharding import PartitionSpec as P

HEAD_DIM = 64
SEQ = 1568


norm_eps = 1e-06


def layer_norm(values, gain, shift):
    center = values - jnp.mean(values, axis=-1, keepdims=True)
    spread = jnp.mean(center * center, axis=-1, keepdims=True)
    return center * lax.rsqrt(spread + norm_eps) * gain + shift


def exact_gelu(values):
    return jax.nn.gelu(values, approximate=False)


def attend_clip(joint_clip):
    heads = joint_clip.reshape(SEQ, 3, -1, HEAD_DIM)
    queries = heads[:, 0]
    keys_all = heads[:, 1]
    values_all = heads[:, 2]
    half = SEQ // 2
    factor = HEAD_DIM ** (-0.5)
    pieces = []
    totals = []
    for block in range(2):
        query_block = queries[block * half : (block + 1) * half]
        scores = (
            jnp.einsum("qhe,khe->hqk", query_block, keys_all, preferred_element_type=jnp.float32)
            * factor
        )
        top = jnp.max(scores, axis=-1, keepdims=True)
        weights = jnp.exp(scores - top)
        total = jnp.sum(weights, axis=-1, keepdims=True)
        chances = (weights / total).astype(jnp.bfloat16)
        mixed = jnp.einsum("hqk,khe->qhe", chances, values_all, preferred_element_type=jnp.float32)
        pieces.append(mixed.reshape(half, -1))
        totals.append((top + jnp.log(total))[:, :, 0])
    return (jnp.concatenate(pieces, axis=0).astype(jnp.bfloat16), jnp.concatenate(totals, axis=1))


def attend_back(joint_clip, upstream_clip, logsum_clip):
    heads = joint_clip.reshape(SEQ, 3, -1, HEAD_DIM)
    queries = heads[:, 0]
    keys_all = heads[:, 1]
    values_all = heads[:, 2]
    upstream = upstream_clip.reshape(SEQ, -1, HEAD_DIM)
    half = SEQ // 2
    factor = HEAD_DIM ** (-0.5)
    key_total = jnp.zeros(keys_all.shape, jnp.float32)
    value_total = jnp.zeros(values_all.shape, jnp.float32)
    query_parts = []
    for block in range(2):
        query_block = queries[block * half : (block + 1) * half]
        upstream_block = upstream[block * half : (block + 1) * half]
        scores = (
            jnp.einsum("qhe,khe->hqk", query_block, keys_all, preferred_element_type=jnp.float32)
            * factor
        )
        chances = jnp.exp(scores - logsum_clip[:, block * half : (block + 1) * half, None])
        rounded = chances.astype(jnp.bfloat16)
        value_total = value_total + jnp.einsum(
            "hqk,qhe->khe", rounded, upstream_block, preferred_element_type=jnp.float32
        )
        pushed = jnp.einsum(
            "qhe,khe->hqk", upstream_block, values_all, preferred_element_type=jnp.float32
        )
        inner = jnp.sum(pushed * chances, axis=-1, keepdims=True)
        score_grad = (chances * (pushed - inner)).astype(jnp.bfloat16)
        query_parts.append(
            jnp.einsum("hqk,khe->qhe", score_grad, keys_all, preferred_element_type=jnp.float32)
            * factor
        )
        key_total = (
            key_total
            + jnp.einsum(
                "hqk,qhe->khe", score_grad, query_block, preferred_element_type=jnp.float32
            )
            * factor
        )
    query_grad = jnp.concatenate(query_parts, axis=0)
    stacked = jnp.stack([query_grad, key_total, value_total], axis=1)
    return stacked.reshape(SEQ, 3, -1).astype(jnp.bfloat16)


def shards(
    tokens,
    attention_gain,
    attention_shift,
    input_weight,
    query_bias,
    value_bias,
    output_weight,
    output_bias,
    feedforward_gain,
    feedforward_shift,
    expand_weight,
    expand_bias,
    reduce_weight,
    reduce_bias,
    cotangent,
):
    rows = tokens.shape[0]
    local_width = input_weight.shape[2]
    share = rows // lax.axis_size("tensor")
    first_row = lax.axis_index("tensor") * share
    inputs = tokens.astype(jnp.float32)
    upstream = cotangent.astype(jnp.float32)
    normed = layer_norm(inputs, attention_gain, attention_shift).astype(jnp.bfloat16)
    joint = jnp.einsum("td,dcf->tcf", normed, input_weight, preferred_element_type=jnp.float32)
    joint_bias = jnp.stack([query_bias, jnp.zeros_like(query_bias), value_bias])
    joint = (joint + joint_bias).astype(jnp.bfloat16)
    clips_joint = joint.reshape(-1, SEQ, 3, local_width)
    attended, logsums = lax.map(attend_clip, clips_joint)
    attended = attended.reshape(rows, local_width)
    own_inputs = lax.dynamic_slice_in_dim(inputs, first_row, share, 0)
    piece = lax.slice_in_dim(attended, 0, share * lax.axis_size("tensor"), axis=0)
    middle = (
        own_inputs
        + lax.psum_scatter(
            jnp.dot(piece, output_weight, preferred_element_type=jnp.float32),
            "tensor",
            scatter_dimension=0,
            tiled=True,
        )
        + output_bias
    )
    normed_two = layer_norm(middle, feedforward_gain, feedforward_shift).astype(jnp.bfloat16)
    gathered = lax.all_gather(normed_two, "tensor", axis=0, tiled=True)
    hidden = jnp.dot(gathered, expand_weight, preferred_element_type=jnp.float32) + expand_bias
    activated = exact_gelu(hidden).astype(jnp.bfloat16)
    piece = lax.dynamic_slice_in_dim(activated, jnp.int32(0), lax.axis_size("tensor") * share, 0)
    result = middle + (
        lax.psum_scatter(
            jnp.dot(piece, reduce_weight, preferred_element_type=jnp.float32).astype(jnp.bfloat16),
            "tensor",
            scatter_dimension=0,
            tiled=True,
        ).astype(jnp.float32)
        + reduce_bias
    )
    block_out = lax.all_gather(result.astype(jnp.bfloat16), "tensor", axis=0, tiled=True)
    reduce_bias_grad = jnp.sum(upstream, axis=0)
    reduce_weight_grad = jnp.einsum(
        "tf,td->fd", activated, cotangent, preferred_element_type=jnp.float32
    )
    activated_grad = jnp.einsum(
        "td,fd->tf", cotangent, reduce_weight, preferred_element_type=jnp.float32
    )
    unused_value, gelu_pull = jax.vjp(exact_gelu, hidden)
    hidden_grad = gelu_pull(activated_grad)[0].astype(jnp.bfloat16)
    expand_bias_grad = jnp.sum(hidden_grad, axis=0, dtype=jnp.float32)
    expand_weight_grad = jnp.einsum(
        "td,tf->df", gathered, hidden_grad, preferred_element_type=jnp.float32
    )
    part = lax.slice_in_dim(hidden_grad, 0, share * lax.axis_size("tensor"), axis=0)
    normed_two_grad = lax.psum_scatter(
        jnp.einsum("tf,df->td", part, expand_weight, preferred_element_type=jnp.float32),
        "tensor",
        scatter_dimension=0,
        tiled=True,
    )
    own_upstream = lax.dynamic_slice_in_dim(upstream, first_row, share, 0)
    unused_second, second_pull = jax.vjp(layer_norm, middle, feedforward_gain, feedforward_shift)
    middle_grad, second_gain_part, second_shift_part = second_pull(normed_two_grad)
    middle_grad = middle_grad + own_upstream
    branch_grad = lax.all_gather(middle_grad.astype(jnp.bfloat16), "tensor", axis=0, tiled=True)
    output_bias_grad = jnp.sum(branch_grad, axis=0, dtype=jnp.float32)
    output_weight_grad = jnp.einsum(
        "tc,td->cd", attended, branch_grad, preferred_element_type=jnp.float32
    )
    attended_grad = jnp.einsum(
        "td,cd->tc", branch_grad, output_weight, preferred_element_type=jnp.float32
    ).astype(jnp.bfloat16)

    def clip_back(items):
        return attend_back(items[0], items[1], items[2])

    joint_grad = lax.map(
        clip_back, (clips_joint, attended_grad.reshape(-1, SEQ, local_width), logsums)
    )
    joint_grad = joint_grad.reshape(rows, 3, local_width)
    query_bias_grad = jnp.sum(joint_grad[:, 0], axis=0, dtype=jnp.float32)
    value_bias_grad = jnp.sum(joint_grad[:, 2], axis=0, dtype=jnp.float32)
    input_weight_grad = jnp.einsum(
        "td,tcf->dcf", normed, joint_grad, preferred_element_type=jnp.float32
    )
    part = joint_grad
    normed_grad = lax.psum_scatter(
        jnp.einsum("tcf,dcf->td", part, input_weight, preferred_element_type=jnp.float32),
        "tensor",
        scatter_dimension=0,
        tiled=True,
    )
    unused_first, first_pull = jax.vjp(layer_norm, own_inputs, attention_gain, attention_shift)
    inputs_grad, first_gain_part, first_shift_part = first_pull(normed_grad)
    inputs_grad = inputs_grad + middle_grad
    tokens_gradient = lax.all_gather(inputs_grad.astype(jnp.bfloat16), "tensor", axis=0, tiled=True)
    (
        input_weight_grad,
        query_bias_grad,
        value_bias_grad,
        output_weight_grad,
        output_bias_grad,
        expand_weight_grad,
        expand_bias_grad,
        reduce_weight_grad,
        reduce_bias_grad,
    ) = lax.psum(
        (
            input_weight_grad,
            query_bias_grad,
            value_bias_grad,
            output_weight_grad,
            output_bias_grad,
            expand_weight_grad,
            expand_bias_grad,
            reduce_weight_grad,
            reduce_bias_grad,
        ),
        "dp",
    )
    first_gain_part, first_shift_part, second_gain_part, second_shift_part = lax.psum(
        (first_gain_part, first_shift_part, second_gain_part, second_shift_part), ("dp", "tensor")
    )
    return (
        block_out,
        tokens_gradient,
        first_gain_part,
        first_shift_part,
        input_weight_grad,
        query_bias_grad,
        value_bias_grad,
        output_weight_grad,
        output_bias_grad,
        second_gain_part,
        second_shift_part,
        expand_weight_grad,
        expand_bias_grad,
        reduce_weight_grad,
        reduce_bias_grad,
    )


def solution(mesh):
    in_specs = (
        P("dp", None),
        P(),
        P(),
        P(None, None, "tensor"),
        P("tensor"),
        P("tensor"),
        P("tensor", None),
        P(),
        P(),
        P(),
        P(None, "tensor"),
        P("tensor"),
        P("tensor", None),
        P(),
        P("dp", None),
    )
    out_specs = (
        P("dp", None),
        P("dp", None),
        P(),
        P(),
        P(None, None, "tensor"),
        P("tensor"),
        P("tensor"),
        P("tensor", None),
        P(),
        P(),
        P(),
        P(None, "tensor"),
        P("tensor"),
        P("tensor", None),
        P(),
    )
    return jax.shard_map(shards, mesh=mesh, in_specs=in_specs, out_specs=out_specs, check_vma=False)
```

profile of v0, /device:TPU:0, one launch (start us, length us, event | category | flops | bytes accessed | tf_op | source)
XLA Modules:
  0.0 1294.4 jit_solution(8680122563296315781)
XLA Ops:
  7.3 2.6 convert_reduce_fusion.2
  9.9 3.1 multiply_reduce_fusion.4
  13.6 7.3 add_convert_fusion.1
  20.9 7.6 copy.41
  28.5 21.3 %multiply_reduce_fusion.2 = (f32[8,784]{1,0:T(8,128)S(1)}, f32[8,784,1568]{2,1,0:T(8,128)}) fusion(bf16[1568,3,8,64]{0,3,2,1:T(8,128)(2,1)} %bitcast.90), kind=kOutput, calls=%fused_computation.12 | convolution fusion | flops 1278478208 | bytes 41984512 | tf_op jit(solution)/shard_map/while/body/eval_jaxpr/qhe,khe->hqk/dot_general | solution.py:35
  49.7 21.1 %multiply_reduce_fusion.3 = (f32[8,784]{1,0:T(8,128)S(1)}, f32[8,784,1568]{2,1,0:T(8,128)}) fusion(bf16[1568,3,8,64]{0,3,2,1:T(8,128)(2,1)} %bitcast.91), kind=kOutput, calls=%fused_computation.13 | convolution fusion | flops 1278478208 | bytes 41984512 | tf_op jit(solution)/shard_map/while/body/eval_jaxpr/qhe,khe->hqk/dot_general | solution.py:35
  70.9 16.7 %fusion.1 = f32[8,784]{1,0:T(8,128)S(1)} fusion(f32[8,784,1568]{2,1,0:T(8,128)} %get-tuple-element.75, f32[8,784]{1,0:T(8,128)S(1)} %get-tuple-element.74), kind=kLoop, calls=%fused_computation.11 | loop fusion | flops 29497216 | bytes 39388160 | tf_op jit(solution)/shard_map/while/body/eval_jaxpr/reduce_sum | solution.py:40
  87.6 15.7 %fusion.20 = bf16[8,64,784]{2,1,0:T(8,128)(2,1)S(1)} fusion(f32[8,784,1568]{2,1,0:T(8,128)} %get-tuple-element.75, f32[8,784]{1,0:T(8,128)S(1)} %fusion.1, f32[8,784]{1,0:T(8,128)S(1)} %get-tuple-element.74, bf16[1568,3,8,64]{0,3,2,1:T(8,128)(2,1)S(1)} %bitcast.98), kind=kOutput, calls=%fused_computation.75 | convolution fusion | flops 1298554880 | bytes 41902080 | tf_op jit(solution)/shard_map/while/body/eval_jaxpr/hqk,khe->qhe/dot_general | solution.py:42
  103.3 16.6 %fusion = f32[8,784]{1,0:T(8,128)S(1)} fusion(f32[8,784,1568]{2,1,0:T(8,128)} %get-tuple-element.77, f32[8,784]{1,0:T(8,128)S(1)} %get-tuple-element.76), kind=kLoop, calls=%fused_computation.10 | loop fusion | flops 29497216 | bytes 39388160 | tf_op jit(solution)/shard_map/while/body/eval_jaxpr/reduce_sum | solution.py:40
  120.0 15.8 %fusion.21 = bf16[8,64,784]{2,1,0:T(8,128)(2,1)S(1)} fusion(f32[8,784,1568]{2,1,0:T(8,128)} %get-tuple-element.77, f32[8,784]{1,0:T(8,128)S(1)} %fusion, f32[8,784]{1,0:T(8,128)S(1)} %get-tuple-element.76, bf16[1568,3,8,64]{0,3,2,1:T(8,128)(2,1)S(1)} %bitcast.99), kind=kOutput, calls=%fused_computation.76 | convolution fusion | flops 1298554880 | bytes 41902080 | tf_op jit(solution)/shard_map/while/body/eval_jaxpr/hqk,khe->qhe/dot_general | solution.py:42
  136.7 4.7 fusion.29
  141.6 5.4 convert_element_type.81
  146.9 2.1 dynamic-slice_reduce_fusion
  149.1 9.4 reduce-scatter.5.cloned.1.call-done
  158.5 4.3 fusion.47
  166.9 14.4 %all-gather.5.cloned.1.call-done = bf16[1568,1024]{1,0:T(8,128)(2,1)} async-done(((bf16[784,1024]{1,0:T(8,128)(2,1)}), bf16[1568,1024]{1,0:T(8,128)(2,1)}) %all-gather.5.cloned.1.call-update) | async-done | bytes 3211280 | tf_op jit(solution)/shard_map/all_gather | solution.py:135
  181.3 10.3 fusion.49
  191.7 38.7 %convert_reduce_fusion = (f32[2048]{0:T(1024)}, bf16[1568,2048]{1,0:T(8,128)(2,1)S(1)}, f32[1568,2048]{1,0:T(8,128)}) fusion(f32[1568,2048]{1,0:T(8,128)S(1)} %fusion.49, f32[2048]{0:T(1024)S(1)} %copy-done.44, bf16[1568,1024]{1,0:T(8,128)(2,1)S(1)} %copy-done.9, bf16[2048,1024]{1,0:T(8,128)(2,1)S(1)} %copy-done.54), kind=kOutput, calls=%fused_computation.22 | convolution fusion | flops 6817511424 | bytes 39534592 | tf_op jit(solution)/shard_map/td,fd->tf/dot_general | solution.py:153
  230.4 2.6 copy-done.63
  233.1 9.1 fusion.50
  242.3 11.1 multiply_convert_fusion.2
  253.4 3.3 copy-done.10
  256.7 8.2 convolution_convert_fusion
  265.0 5.4 convert_element_type.92
  270.4 5.6 multiply_reduce_fusion.5
  277.4 5.7 fusion.46
  284.9 3.4 fusion.33
  288.4 13.5 %all-gather.9.cloned.1.call-done = bf16[1568,1024]{1,0:T(8,128)(2,1)} async-done(((bf16[784,1024]{1,0:T(8,128)(2,1)}), bf16[1568,1024]{1,0:T(8,128)(2,1)}) %all-gather.9.cloned.1.call-update) | async-done | bytes 3211280 | tf_op jit(solution)/shard_map/all_gather | solution.py:173
  301.9 4.1 convolution_convert_fusion.1
  307.3 2.4 copy.42
  309.7 27.8 %multiply_reduce_fusion.1 = (f32[8,784]{1,0:T(8,128)S(1)}, f32[8,784,1568]{2,1,0:T(8,128)}) fusion(f32[8,784,1568]{2,1,0:T(8,128)} %get-tuple-element.77, f32[8,784]{1,0:T(8,128)S(1)} %log_add_fusion.1, bf16[784,8,64]{0,2,1:T(8,128)(2,1)} %bitcast.105, bf16[1568,3,8,64]{0,3,2,1:T(8,128)(2,1)} %bitcast.92), kind=kOutput, calls=%fused_computation.4 | convolution fusion | flops 1298147200 | bytes 83756032 | tf_op jit(solution)/shard_map/while/body/eval_jaxpr/qhe,khe->hqk/dot_general | solution.py:71
  337.4 34.0 %multiply_convert_fusion.1 = bf16[8,784,1568]{2,1,0:T(8,128)(2,1)} fusion(f32[8,784,1568]{2,1,0:T(8,128)} %get-tuple-element.79, f32[8,784,1568]{2,1,0:T(8,128)} %get-tuple-element.77, f32[8,784]{1,0:T(8,128)S(1)} %get-tuple-element.78, f32[8,784]{1,0:T(8,128)S(1)} %log_add_fusion.1), kind=kLoop, calls=%fused_computation.3 | loop fusion | flops 49172480 | bytes 98395136 | tf_op jit(solution)/shard_map/while/body/eval_jaxpr/convert_element_type | solution.py:75
  371.5 12.8 fusion.22
  384.3 12.3 fusion.32
  396.6 2.2 copy.43
  398.8 18.9 %fusion.4 = f32[8,64,1568]{2,1,0:T(8,128)} fusion(bf16[784,8,64]{0,2,1:T(8,128)(2,1)} %bitcast.103, f32[8,784,1568]{2,1,0:T(8,128)} %get-tuple-element.75, f32[8,784]{1,0:T(8,128)S(1)} %log_add_fusion), kind=kOutput, calls=%fused_computation.16 | convolution fusion | flops 1288318976 | bytes 43377152 | tf_op jit(solution)/shard_map/while/body/eval_jaxpr/hqk,qhe->khe/dot_general | solution.py:68
  417.7 27.8 %multiply_reduce_fusion = (f32[8,784]{1,0:T(8,128)S(1)}, f32[8,784,1568]{2,1,0:T(8,128)}) fusion(f32[8,784,1568]{2,1,0:T(8,128)} %get-tuple-element.75, f32[8,784]{1,0:T(8,128)S(1)} %log_add_fusion, bf16[784,8,64]{0,2,1:T(8,128)(2,1)} %bitcast.104, bf16[1568,3,8,64]{0,3,2,1:T(8,128)(2,1)} %bitcast.95), kind=kOutput, calls=%fused_computation.1 | convolution fusion | flops 1298147200 | bytes 83756032 | tf_op jit(solution)/shard_map/while/body/eval_jaxpr/qhe,khe->hqk/dot_general | solution.py:71
  445.5 18.9 %add_convert_fusion.3 = bf16[8,64,1568]{2,1,0:T(8,128)(2,1)} fusion(f32[8,64,1568]{2,1,0:T(8,128)} %fusion.4, bf16[784,8,64]{0,2,1:T(8,128)(2,1)} %bitcast.106, f32[8,784,1568]{2,1,0:T(8,128)} %get-tuple-element.77, f32[8,784]{1,0:T(8,128)S(1)} %log_add_fusion.1), kind=kOutput, calls=%fused_computation.50 | convolution fusion | flops 1289924608 | bytes 44982784 | tf_op jit(solution)/shard_map/while/body/eval_jaxpr/hqk,qhe->khe/dot_general | solution.py:68
  464.4 3.6 copy.46
  467.9 34.0 %multiply_convert_fusion = bf16[8,784,1568]{2,1,0:T(8,128)(2,1)} fusion(f32[8,784,1568]{2,1,0:T(8,128)} %get-tuple-element.81, f32[8,784,1568]{2,1,0:T(8,128)} %get-tuple-element.75, f32[8,784]{1,0:T(8,128)S(1)} %get-tuple-element.80, f32[8,784]{1,0:T(8,128)S(1)} %log_add_fusion), kind=kLoop, calls=%fused_computation | loop fusion | flops 49172480 | bytes 98395136 | tf_op jit(solution)/shard_map/while/body/eval_jaxpr/convert_element_type | solution.py:75
  502.0 13.0 %fusion.23 = bf16[784,8,64]{0,2,1:T(8,128)(2,1)} fusion(bf16[8,784,1568]{2,1,0:T(8,128)(2,1)} %multiply_convert_fusion, bf16[1568,3,8,64]{0,3,2,1:T(8,128)(2,1)} %bitcast.96), kind=kOutput, calls=%fused_computation.78 | convolution fusion | flops 1259618304 | bytes 23379968 | tf_op jit(solution)/shard_map/while/body/eval_jaxpr/hqk,khe->qhe/dot_general | solution.py:77
  514.9 13.2 %multiply_convert_fusion.3 = bf16[8,64,1568]{2,1,0:T(8,128)(2,1)} fusion(f32[8,64,1568]{2,1,0:T(8,128)} %fusion.32, bf16[8,784,1568]{2,1,0:T(8,128)(2,1)} %multiply_convert_fusion, bf16[1568,3,8,64]{0,3,2,1:T(8,128)(2,1)} %bitcast.97), kind=kOutput, calls=%fused_computation.51 | convolution fusion | flops 1261223936 | bytes 26804224 | tf_op jit(solution)/shard_map/while/body/eval_jaxpr/hqk,qhe->khe/dot_general | solution.py:82
  528.1 3.6 copy.45
  531.7 3.2 pad_maximum_fusion.4
  534.9 3.6 copy.44
  538.5 8.7 convolution_bitcast_fusion
  548.0 13.2 %fusion.52 = f32[2048,1024]{1,0:T(8,128)} fusion(bf16[1568,2048]{1,0:T(8,128)(2,1)} %copy-done.10, bf16[1568,1024]{1,0:T(8,128)(2,1)} %param.29), kind=kOutput, calls=%fused_computation.119 | convolution fusion | flops 6576668672 | bytes 18022400 | tf_op jit(solution)/shard_map/tf,td->fd/dot_general | solution.py:150
  562.7 4.1 multiply_reduce_fusion.6
  566.8 3.1 fusion.45
  570.0 3.8 add_convert_fusion.4
  573.8 14.1 %fusion.51 = f32[1024,2048]{1,0:T(8,128)} fusion(bf16[1568,1024]{1,0:T(8,128)(2,1)} %all-gather.5.cloned.1.call-done, bf16[1568,2048]{1,0:T(8,128)(2,1)} %copy-done.63), kind=kOutput, calls=%fused_computation.118 | convolution fusion | flops 6576668672 | bytes 18022400 | tf_op jit(solution)/shard_map/td,tf->df/dot_general | solution.py:159
  588.1 3.4 fusion.28
  593.1 9.1 fusion.19
  602.3 2.5 convert_reduce_fusion.5
  604.8 1.8 convert_reduce_fusion.3
  606.6 1.8 convert_reduce_fusion.4
  608.3 3.2 convert_reduce_fusion.1
  611.5 82.4 %all-reduce.1 = (f32[512]{0:T(512)}, f32[512]{0:T(512)}, f32[1024]{0:T(1024)}, f32[2048]{0:T(1024)}, f32[1024]{0:T(1024)}) all-reduce(f32[512]{0:T(512)S(1)} %convert_reduce_fusion.4, f32[512]{0:T(512)S(1)} %convert_reduce_fusion.3, f32[1024]{0:T(1024)S(1)} %convert_reduce_fusion.1, ...), channel_id=1, replica_groups=mesh['dp'=16,'tensor'=2] {'dp'}, use_global_device_ids=true, to_apply=%region_26.27 | all-reduce | flops 5120 | bytes 40960 | tf_op jit(solution)/shard_map/psum | solution.py:215
  694.0 41.3 %all-reduce = (f32[1024]{0:T(1024)}, f32[1024]{0:T(1024)}, f32[1024]{0:T(1024)}, f32[1024]{0:T(1024)}) all-reduce(f32[1024]{0:T(1024)S(1)} %get-tuple-element.42, f32[1024]{0:T(1024)S(1)} %get-tuple-element.47, f32[1024]{0:T(1024)S(1)} %copy-done.42, f32[1024]{0:T(1024)S(1)} %copy-done.43), channel_id=1, replica_groups=mesh['dp'=16,'tensor'=2] {'dp','tensor'}, use_global_device_ids=true, to_apply=%region_21.22 | all-reduce | flops 4096 | bytes 32768 | tf_op jit(solution)/shard_map/psum | solution.py:229
  735.2 530.3 %all-reduce.5.cloned.1.call-done = (f32[1024,3,512]{2,0,1:T(8,128)}, f32[512,1024]{1,0:T(8,128)}, f32[1024,2048]{1,0:T(8,128)}, f32[2048,1024]{1,0:T(8,128)}) async-done(((f32[1024,3,512]{2,0,1:T(8,128)}, f32[512,1024]{1,0:T(8,128)}, f32[1024,2048]{1,0:T(8,128)}, f32[2048,1024]{1,0:T(8,128)}), (f32[1024,3,512]{2,0,1:T(8,128)}, f32[512,1024]{1,0:T(8,128)}, f32[1024,2048]{1,0:T(8,128)}, ...) | async-done | bytes 25165840 | tf_op jit(solution)/shard_map/psum | solution.py:215
  1265.6 4.1 copy.53
  1272.6 3.2 copy.55
  1278.9 4.2 copy.57
  1284.2 3.4 copy.58
  (183 shorter events, 21.6 us)
Async XLA Ops:
  7.2 6.4 copy-start
  7.2 5.9 copy-start.51
  7.2 5.9 copy-start.52
  7.2 6.4 copy-start.40
  7.2 6.4 copy-start.57
  7.2 151.3 %reduce-scatter.5.cloned.1.call-start = ((), (), s32[]{:S(2)}) async-start(), calls=%async_computation.4 | async-start | bytes 9633792 | tf_op jit(solution)/shard_map/reduce_scatter | solution.py:126
  7.3 6.3 copy-start.5
  49.7 37.9 %copy-start.17 = (f32[8,784]{1,0:T(8,128)}, f32[8,784]{1,0:T(8,128)S(1)}, u32[]{:S(2)}) copy-start(f32[8,784]{1,0:T(8,128)S(1)} %get-tuple-element.74) | copy-start | bytes 75268
  70.9 49.1 %copy-start.19 = (f32[8,784]{1,0:T(8,128)}, f32[8,784]{1,0:T(8,128)S(1)}, u32[]{:S(2)}) copy-start(f32[8,784]{1,0:T(8,128)S(1)} %get-tuple-element.76) | copy-start | bytes 75268
  70.9 16.8 %copy-start.1 = (bf16[1568,3,512]{0,2,1:T(8,128)(2,1)S(1)}, bf16[1568,3,512]{0,2,1:T(8,128)(2,1)}, u32[]{:S(2)}) copy-start(bf16[1568,3,512]{0,2,1:T(8,128)(2,1)} %copy.41) | copy-start | bytes 14450692
  87.6 15.7 %copy-start.21 = (f32[8,784]{1,0:T(8,128)}, f32[8,784]{1,0:T(8,128)S(1)}, u32[]{:S(2)}) copy-start(f32[8,784]{1,0:T(8,128)S(1)} %fusion.1) | copy-start | bytes 75268
  103.3 32.4 %copy-start.59 = (bf16[8,64,784]{2,1,0:T(8,128)(2,1)}, bf16[8,64,784]{2,1,0:T(8,128)(2,1)S(1)}, u32[]{:S(2)}) copy-start(bf16[8,64,784]{2,1,0:T(8,128)(2,1)S(1)} %fusion.20) | copy-start | bytes 2408452
  119.9 15.8 %copy-start.23 = (f32[8,784]{1,0:T(8,128)}, f32[8,784]{1,0:T(8,128)S(1)}, u32[]{:S(2)}) copy-start(f32[8,784]{1,0:T(8,128)S(1)} %fusion) | copy-start | bytes 75268
  120.0 16.8 %copy-start.56 = (bf16[512,1024]{1,0:T(8,128)(2,1)S(1)}, bf16[512,1024]{1,0:T(8,128)(2,1)}, u32[]{:S(2)}) copy-start(bf16[512,1024]{1,0:T(8,128)(2,1)} %param.21) | copy-start | bytes 3145732
  141.5 39.8 %all-gather.5.cloned.1.call-start = ((), (), s32[]{:S(2)}) async-start(), calls=%async_computation.5 | async-start | bytes 4816896 | tf_op jit(solution)/shard_map/all_gather | solution.py:135
  141.6 17.0 %copy-start.48 = (f32[1024]{0:T(1024)S(1)}, f32[1024]{0:T(1024)}, u32[]{:S(2)}) copy-start(f32[1024]{0:T(1024)} %param.22) | copy-start | bytes 12292
  149.1 14.2 %copy-start.27 = (f32[784]{0:T(1024)}, f32[784]{0:T(1024)S(1)}, u32[]{:S(2)}) copy-start(f32[784]{0:T(1024)S(1)} %broadcast_multiply_fusion.1) | copy-start | bytes 9412
  149.1 16.0 %copy-start.34 = (f32[1024]{0:T(1024)S(1)}, f32[1024]{0:T(1024)}, u32[]{:S(2)}) copy-start(f32[1024]{0:T(1024)} %param.23) | copy-start | bytes 12292
  149.1 16.0 %copy-start.49 = (f32[1024]{0:T(1024)S(1)}, f32[1024]{0:T(1024)}, u32[]{:S(2)}) copy-start(f32[1024]{0:T(1024)} %param.24) | copy-start | bytes 12292
  166.9 24.8 %copy-start.44 = (f32[2048]{0:T(1024)S(1)}, f32[2048]{0:T(1024)}, u32[]{:S(2)}) copy-start(f32[2048]{0:T(1024)} %param.26) | copy-start | bytes 24580
  166.9 103.5 %reduce-scatter.9.cloned.1.call-start = ((), (), s32[]{:S(2)}) async-start(), calls=%async_computation.8 | async-start | bytes 9633792 | tf_op jit(solution)/shard_map/reduce_scatter | solution.py:163
  181.3 10.3 copy-start.9
  181.3 10.3 copy-start.54
  191.7 38.8 %copy-start.8 = (f32[1568,2048]{1,0:T(8,128)}, f32[1568,2048]{1,0:T(8,128)S(1)}, u32[]{:S(2)}) copy-start(f32[1568,2048]{1,0:T(8,128)S(1)} %fusion.49) | copy-start | bytes 38535172
  191.7 41.4 %copy-start.53 = (bf16[1024,2048]{1,0:T(8,128)(2,1)S(1)}, bf16[1024,2048]{1,0:T(8,128)(2,1)}, u32[]{:S(2)}) copy-start(bf16[1024,2048]{1,0:T(8,128)(2,1)} %param.25) | copy-start | bytes 12582916
  242.2 35.2 %reduce-scatter.7.cloned.1.call-start = ((), (), s32[]{:S(2)}) async-start(), calls=%async_computation.6 | async-start | bytes 4816896 | tf_op jit(solution)/shard_map/reduce_scatter | solution.py:140
  242.3 14.4 %copy-start.55 = (bf16[2048,1024]{1,0:T(8,128)(2,1)S(1)}, bf16[2048,1024]{1,0:T(8,128)(2,1)}, u32[]{:S(2)}) copy-start(bf16[2048,1024]{1,0:T(8,128)(2,1)} %param.27) | copy-start | bytes 12582916
  264.9 5.5 copy-start.26
  264.9 5.5 copy-start.30
  264.9 5.5 copy-start.35
  264.9 11.1 copy-start.37
  264.9 12.5 copy-start.50
  264.9 37.0 %all-gather.9.cloned.1.call-start = ((), (), s32[]{:S(2)}) async-start(), calls=%async_computation.9 | async-start | bytes 4816896 | tf_op jit(solution)/shard_map/all_gather | solution.py:173
  283.2 5.2 copy-start.18
  283.2 5.2 copy-start.22
  283.2 5.2 copy-start.20
  283.2 5.2 copy-start.24
  288.3 274.4 %reduce-scatter.11.cloned.1.call-start = ((), (), s32[]{:S(2)}) async-start(), calls=%async_computation.10 | async-start | bytes 9633792 | tf_op jit(solution)/shard_map/reduce_scatter | solution.py:195
  547.2 57.6 %all-gather.7.cloned.1.call-start = ((), (), s32[]{:S(2)}) async-start(), calls=%async_computation.7 | async-start | bytes 4816896 | tf_op jit(solution)/shard_map/all_gather | solution.py:148
  547.9 14.7 %copy-start.28 = (f32[784]{0:T(1024)S(1)}, f32[784]{0:T(1024)}, u32[]{:S(2)}) copy-start(f32[784]{0:T(1024)} %copy-done.27) | copy-start | bytes 9412
  548.0 14.7 %copy-start.41 = (f32[1024]{0:T(1024)S(1)}, f32[1024]{0:T(1024)}, u32[]{:S(2)}) copy-start(f32[1024]{0:T(1024)} %param.16) | copy-start | bytes 12292
  548.0 187.3 %all-gather.11.cloned.1.call-start = ((), (), s32[]{:S(2)}) async-start(), calls=%async_computation.11 | async-start | bytes 4816896 | tf_op jit(solution)/shard_map/all_gather | solution.py:204
  562.7 4.2 copy-start.7
  573.8 691.8 %all-reduce.5.cloned.1.call-start = ((), (), s32[]{:S(2)}) async-start(), calls=%async_computation.12 | async-start | bytes 50331648 | tf_op jit(solution)/shard_map/psum | solution.py:215
  573.8 14.2 %copy-start.11 = (bf16[1568,1024]{1,0:T(8,128)(2,1)S(1)}, bf16[1568,1024]{1,0:T(8,128)(2,1)}, u32[]{:S(2)}) copy-start(bf16[1568,1024]{1,0:T(8,128)(2,1)} %all-gather.9.cloned.1.call-done) | copy-start | bytes 9633796
  573.8 14.2 %copy-start.60 = (bf16[8,64,784]{2,1,0:T(8,128)(2,1)S(1)}, bf16[8,64,784]{2,1,0:T(8,128)(2,1)}, u32[]{:S(2)}) copy-start(bf16[8,64,784]{2,1,0:T(8,128)(2,1)} %copy-done.59) | copy-start | bytes 2408452
  573.8 14.2 %copy-start.62 = (bf16[8,64,784]{2,1,0:T(8,128)(2,1)S(1)}, bf16[8,64,784]{2,1,0:T(8,128)(2,1)}, u32[]{:S(2)}) copy-start(bf16[8,64,784]{2,1,0:T(8,128)(2,1)} %copy-done.61) | copy-start | bytes 2408452
  588.0 3.5 copy-start.6
  588.0 4.4 copy-start.15
  588.0 5.1 copy-start.16
  588.0 5.1 copy-start.39
  588.0 5.1 copy-start.46
  588.1 5.1 copy-start.58
  602.2 9.3 copy-start.47
  602.2 91.7 %copy-start.42 = (f32[1024]{0:T(1024)S(1)}, f32[1024]{0:T(1024)}, u32[]{:S(2)}) copy-start(f32[1024]{0:T(1024)} %get-tuple-element.44) | copy-start | bytes 12292
  602.3 91.7 %copy-start.43 = (f32[1024]{0:T(1024)S(1)}, f32[1024]{0:T(1024)}, u32[]{:S(2)}) copy-start(f32[1024]{0:T(1024)} %get-tuple-element.46) | copy-start | bytes 12292
  1265.6 4.1 copy-start.12
  1265.6 5.8 slice-start.4
  1265.6 7.0 slice-start.5
  1269.7 8.1 slice-start.2
  1272.6 3.8 copy-start.13
  1272.6 6.2 slice-start.3
  1276.4 6.7 slice-start
  1278.9 5.4 slice-start.1
  (15 other events, 29.6 us)
Sparse Core Ops, SparseCore 0:
  141.6 16.8 reduce-scatter.4
  167.0 14.2 all-gather.4
  242.3 15.3 reduce-scatter.8
  265.0 12.3 reduce-scatter.6
  288.4 13.4 all-gather.8
  547.3 15.3 reduce-scatter.10
  564.2 14.2 all-gather.6
  580.7 13.3 all-gather.10
  602.4 663.1 all-reduce.4
where the time goes:
time: 1300 us; the launch traced here: 1290 us
  waiting for transfers between devices  571 us (44%)
  matrix products  349 us (27%)
  other arithmetic  176 us (14%)
  blocking collectives  124 us (10%)
  local copies, waits for them, and re-layouts  59.6 us (5%)
  between operations  14.8 us (1%)
    psum x1, waiting for transfers between devices, shards(): lax.psum((input_weight_grad, query_bias_grad, value_bias_grad, output_wei...  530 us
    psum x1, blocking collectives, shards(): lax.psum((input_weight_grad, query_bias_grad, value_bias_grad, output_wei...  82.4 us
    convert_element_type x2, other arithmetic, attend_back(): score_grad = (chances * (pushed - inner)).astype(jnp.bfloat16)  68.1 us
    dot_general x2, matrix products, attend_back(): jnp.einsum('qhe,khe->hqk', upstream_block, values_all, preferred_element_...  55.6 us
    dot_general x2, matrix products, attend_clip(): jnp.einsum('qhe,khe->hqk', query_block, keys_all, preferred_element_type=...  42.4 us
    psum x1, blocking collectives, shards(): lax.psum((first_gain_part, first_shift_part, second_gain_part, second_shi...  41.3 us
    dot_general x1, matrix products, shards(): jnp.einsum('td,fd->tf', cotangent, reduce_weight, preferred_element_type=...  38.7 us
    dot_general x2, matrix products, attend_back(): jnp.einsum('hqk,qhe->khe', rounded, upstream_block, preferred_element_typ...  37.8 us
  transfers between devices with their start and end apart: 9, of which 6 were waited for; matrix products, arithmetic and copies ran while one was open for 8% of the time, Pallas kernels for 0%

commit v1 on v0

v1 whole, which is shorter than its diff:
```python
import functools

import jax
import jax.numpy as jnp
from jax import lax
from jax.experimental import pallas as pl
from jax.experimental.pallas import tpu as pltpu
from jax.sharding import PartitionSpec as P

HEAD_DIM = 64
SEQ = 1568
PAIR = 2 * HEAD_DIM
F32 = jnp.float32
BF16 = jnp.bfloat16
EXP_SCALE = 0.125 * 1.4426950408889634

norm_eps = 1e-06


def layer_norm(values, gain, shift):
    center = values - jnp.mean(values, axis=-1, keepdims=True)
    spread = jnp.mean(center * center, axis=-1, keepdims=True)
    return center * lax.rsqrt(spread + norm_eps) * gain + shift


def exact_gelu(values):
    return jax.nn.gelu(values, approximate=False)


def dot_nn(a, b):
    return lax.dot_general(a, b, (((1,), (0,)), ((), ())), preferred_element_type=F32)


def dot_nt(a, b):
    return lax.dot_general(a, b, (((1,), (1,)), ((), ())), preferred_element_type=F32)


def dot_tn(a, b):
    return lax.dot_general(a, b, (((0,), (0,)), ((), ())), preferred_element_type=F32)


def attend_kernel(q_ref, k_ref, v_ref, out_ref, inverse_ref, weights_ref):
    low_half = lax.broadcasted_iota(jnp.int32, (1, PAIR), 1) < HEAD_DIM
    zero = jnp.zeros((), BF16)
    keys, values, queries = k_ref[...], v_ref[...], q_ref[...]
    mixed, inverses = [], []
    for head in range(2):
        own_keys = jnp.where(low_half if head == 0 else ~low_half, keys, zero)
        scores = dot_nt(queries, own_keys)
        top = jnp.max(scores, axis=1, keepdims=True)
        weights = jnp.exp2((scores - top) * EXP_SCALE)
        inverse = 1.0 / jnp.sum(weights, axis=1, keepdims=True)
        weights = weights.astype(BF16)
        weights_ref[head] = weights
        mixed.append(dot_nn(weights, values) * inverse)
        inverses.append(inverse)
    out_ref[...] = jnp.where(low_half, mixed[0], mixed[1]).astype(BF16)
    inverse_ref[...] = jnp.where(low_half, inverses[0], inverses[1])


def attend(queries, keys, values, block=224):
    rows, width = queries.shape
    pairs = width // PAIR
    tile = pl.BlockSpec((block, PAIR), lambda p, i: (i, p))
    whole = pl.BlockSpec((rows, PAIR), lambda p, i: (0, p))
    return pl.pallas_call(
        attend_kernel,
        grid=(pairs, rows // block),
        in_specs=[tile, whole, whole],
        out_specs=[tile, tile, pl.BlockSpec((2, block, rows), lambda p, i: (p, i, 0))],
        out_shape=[
            jax.ShapeDtypeStruct((rows, width), BF16),
            jax.ShapeDtypeStruct((rows, width), F32),
            jax.ShapeDtypeStruct((2 * pairs, rows, rows), BF16),
        ],
        compiler_params=pltpu.CompilerParams(vmem_limit_bytes=60 << 20),
        cost_estimate=pl.CostEstimate(
            flops=8 * pairs * rows * rows * HEAD_DIM * 4,
            bytes_accessed=4 * pairs * rows * rows,
            transcendentals=2 * pairs * rows * rows,
        ),
        name="attend",
    )(queries, keys, values)


def attend_back_kernel(
    q_ref, k_ref, v_ref, g_ref, o_ref, inverse_ref, weights_ref, dq_ref, dk_ref, dv_ref, dk_sum, dv_sum
):
    step, steps = pl.program_id(1), pl.num_programs(1)
    low_half = lax.broadcasted_iota(jnp.int32, (1, PAIR), 1) < HEAD_DIM
    zero = jnp.zeros((), BF16)

    @pl.when(step == 0)
    def _():
        dk_sum[...] = jnp.zeros_like(dk_sum)
        dv_sum[...] = jnp.zeros_like(dv_sum)

    keys, values, queries = k_ref[...], v_ref[...], q_ref[...]
    grads = (g_ref[...].astype(F32) * inverse_ref[...]).astype(BF16)
    products = grads.astype(F32) * o_ref[...].astype(F32)
    query_grad = None
    for head in range(2):
        own = low_half if head == 0 else ~low_half
        inner = jnp.sum(jnp.where(own, products, 0.0), axis=1, keepdims=True)
        weights = weights_ref[head]
        pushed = dot_nt(grads, jnp.where(own, values, zero))
        score_grad = (weights.astype(F32) * (pushed - inner)).astype(BF16)
        part = dot_nn(score_grad, jnp.where(own, keys, zero))
        query_grad = part if query_grad is None else query_grad + part
        dv_sum[...] += dot_tn(weights, jnp.where(own, grads, zero))
        dk_sum[...] += dot_tn(score_grad, jnp.where(own, queries, zero))
    dq_ref[...] = (query_grad * 0.125).astype(BF16)

    @pl.when(step == steps - 1)
    def _():
        dk_ref[...] = (dk_sum[...] * 0.125).astype(BF16)
        dv_ref[...] = dv_sum[...].astype(BF16)


def attend_back(queries, keys, values, grads, outs, inverse, weights, block=224):
    rows, width = queries.shape
    pairs = width // PAIR
    tile = pl.BlockSpec((block, PAIR), lambda p, i: (i, p))
    whole = pl.BlockSpec((rows, PAIR), lambda p, i: (0, p))
    return pl.pallas_call(
        attend_back_kernel,
        grid=(pairs, rows // block),
        in_specs=[tile, whole, whole, tile, tile, tile, pl.BlockSpec((2, block, rows), lambda p, i: (p, i, 0))],
        out_specs=[tile, whole, whole],
        out_shape=[jax.ShapeDtypeStruct((rows, width), BF16)] * 3,
        scratch_shapes=[pltpu.VMEM((rows, PAIR), F32)] * 2,
        compiler_params=pltpu.CompilerParams(vmem_limit_bytes=60 << 20),
        cost_estimate=pl.CostEstimate(
            flops=16 * pairs * rows * rows * HEAD_DIM * 4,
            bytes_accessed=4 * pairs * rows * rows,
            transcendentals=0,
        ),
        name="attend_back",
    )(queries, keys, values, grads, outs, inverse, weights)


def column_sum(values):
    return jnp.sum(values, axis=0, dtype=F32)


def shards(
    tokens,
    attention_gain,
    attention_shift,
    input_weight,
    query_bias,
    value_bias,
    output_weight,
    output_bias,
    feedforward_gain,
    feedforward_shift,
    expand_weight,
    expand_bias,
    reduce_weight,
    reduce_bias,
    cotangent,
):
    rows = tokens.shape[0]
    share = rows // lax.axis_size("tensor")
    first_row = lax.axis_index("tensor") * share

    def scatter(values):
        return lax.psum_scatter(values, "tensor", scatter_dimension=0, tiled=True)

    def gather(values):
        return lax.all_gather(values, "tensor", axis=0, tiled=True)

    stacked_weight = jnp.transpose(input_weight, (1, 0, 2))
    inputs = tokens.astype(F32)
    upstream = cotangent.astype(F32)
    normed = layer_norm(inputs, attention_gain, attention_shift).astype(BF16)
    queries = (dot_nn(normed, stacked_weight[0]) + query_bias).astype(BF16)
    keys = dot_nn(normed, stacked_weight[1]).astype(BF16)
    values = (dot_nn(normed, stacked_weight[2]) + value_bias).astype(BF16)
    attended, inverse, weights = attend(queries, keys, values)
    own_inputs = lax.dynamic_slice_in_dim(inputs, first_row, share, 0)
    middle = own_inputs + scatter(dot_nn(attended, output_weight).astype(BF16)).astype(F32) + output_bias
    normed_two = layer_norm(middle, feedforward_gain, feedforward_shift).astype(BF16)
    gathered = gather(normed_two)
    hidden = dot_nn(gathered, expand_weight) + expand_bias
    activated = exact_gelu(hidden).astype(BF16)
    result = middle + (scatter(dot_nn(activated, reduce_weight).astype(BF16)).astype(F32) + reduce_bias)
    block_out = gather(result.astype(BF16))
    reduce_bias_grad = column_sum(upstream)
    reduce_weight_grad = dot_tn(activated, cotangent).astype(BF16)
    activated_grad = dot_nt(cotangent, reduce_weight)
    _, gelu_pull = jax.vjp(exact_gelu, hidden)
    hidden_grad = gelu_pull(activated_grad)[0].astype(BF16)
    expand_bias_grad = column_sum(hidden_grad)
    expand_weight_grad = dot_tn(gathered, hidden_grad).astype(BF16)
    normed_two_grad = scatter(dot_nt(hidden_grad, expand_weight).astype(BF16)).astype(F32)
    own_upstream = lax.dynamic_slice_in_dim(upstream, first_row, share, 0)
    _, second_pull = jax.vjp(layer_norm, middle, feedforward_gain, feedforward_shift)
    middle_grad, second_gain_part, second_shift_part = second_pull(normed_two_grad)
    middle_grad = middle_grad + own_upstream
    branch_grad = gather(middle_grad.astype(BF16))
    output_bias_grad = column_sum(branch_grad)
    output_weight_grad = dot_tn(attended, branch_grad).astype(BF16)
    attended_grad = dot_nt(branch_grad, output_weight).astype(BF16)
    joint_grad = attend_back(queries, keys, values, attended_grad, attended, inverse, weights)
    query_bias_grad = column_sum(joint_grad[0])
    value_bias_grad = column_sum(joint_grad[2])
    input_weight_grad = tuple(dot_tn(normed, part).astype(BF16) for part in joint_grad)
    normed_grad = sum(dot_nt(part, stacked_weight[i]) for i, part in enumerate(joint_grad))
    normed_grad = scatter(normed_grad.astype(BF16)).astype(F32)
    _, first_pull = jax.vjp(layer_norm, own_inputs, attention_gain, attention_shift)
    inputs_grad, first_gain_part, first_shift_part = first_pull(normed_grad)
    tokens_gradient = gather((inputs_grad + middle_grad).astype(BF16))

    norm_parts = lax.psum(
        jnp.stack([first_gain_part, first_shift_part, second_gain_part, second_shift_part]), "tensor"
    )
    small = [
        norm_parts.reshape(-1),
        reduce_bias_grad,
        output_bias_grad,
        query_bias_grad,
        value_bias_grad,
        expand_bias_grad,
    ]
    sizes = [part.shape[0] for part in small]
    sums = lax.psum(
        (
            *input_weight_grad,
            output_weight_grad,
            expand_weight_grad,
            reduce_weight_grad,
            jnp.concatenate(small).astype(BF16),
        ),
        "dp",
    )
    sums = [part.astype(F32) for part in sums]
    ends = [sum(sizes[: i + 1]) for i in range(len(sizes))]
    parts = [sums[6][end - size : end] for size, end in zip(sizes, ends)]
    norms = parts[0].reshape(4, -1)
    return (
        block_out,
        tokens_gradient,
        norms[0],
        norms[1],
        jnp.transpose(jnp.stack(sums[:3]), (1, 0, 2)),
        parts[3],
        parts[4],
        sums[3],
        parts[2],
        norms[2],
        norms[3],
        sums[4],
        parts[5],
        sums[5],
        parts[1],
    )


def solution(mesh):
    in_specs = (
        P("dp", None),
        P(),
        P(),
        P(None, None, "tensor"),
        P("tensor"),
        P("tensor"),
        P("tensor", None),
        P(),
        P(),
        P(),
        P(None, "tensor"),
        P("tensor"),
        P("tensor", None),
        P(),
        P("dp", None),
    )
    out_specs = (
        P("dp", None),
        P("dp", None),
        P(),
        P(),
        P(None, None, "tensor"),
        P("tensor"),
        P("tensor"),
        P("tensor", None),
        P(),
        P(),
        P(),
        P(None, "tensor"),
        P("tensor"),
        P("tensor", None),
        P(),
    )
    return jax.shard_map(shards, mesh=mesh, in_specs=in_specs, out_specs=out_specs, check_vma=False)
```

time: 1300 us -> 750 us (0.58)
  waiting for transfers between devices: 571 us -> 308 us
  matrix products: 349 us -> 132 us
  Pallas kernels: 0 us -> 109 us
  other arithmetic: 176 us -> 73.5 us
  local copies, waits for them, and re-layouts: 59.6 us -> 18.1 us
  blocking collectives: 124 us -> 85.9 us
    psum x1, waiting for transfers between devices: 530 us -> 264 us  [shards(): lax.psum((*input_weight_grad, output_weight_grad, expand_weight_grad, red...]
    dot_general x24 -> x18, matrix products: 349 us -> 132 us  [the longest x6 61.6 us: dot_nt(): lax.dot_general(a, b, (((1,), (1,)), ((), ())), preferred_element_type=F32)]
    pallas_call x0 -> x2, Pallas kernels: none -> 109 us  [the longest x1 60.3 us: attend_back(): pl.pallas_call(attend_back_kernel, grid=(pairs, rows // block), in_specs=...]
    convert_element_type x8 -> x9, other arithmetic: 98.8 us -> 39.2 us  [the longest x3 14 us: shards(): sums = [part.astype(F32) for part in sums]]
    psum x2, blocking collectives: 124 us -> 85.9 us  [the longest x1 82.5 us: shards(): lax.psum((*input_weight_grad, output_weight_grad, expand_weight_grad, red...]
    reduce_sum x6 -> x4, other arithmetic: 42.6 us -> 7.01 us  [column_sum(): return jnp.sum(values, axis=0, dtype=F32)]
    unnamed x146 -> x109, local copies, waits for them, and re-layouts: 35.3 us -> 16.3 us
  transfers between devices with their start and end apart: 9 -> 9, of which waited for: 6 -> 5; matrix products, arithmetic and copies ran while one was open for 8% -> 12% of each run, Pallas kernels for 0% -> 0%
where the time goes in v1:
time: 750 us; the launch traced here: 742 us
  waiting for transfers between devices  308 us (41%)
  matrix products  132 us (18%)
  Pallas kernels  109 us (15%)
  blocking collectives  85.9 us (11%)
  other arithmetic  73.5 us (10%)
  local copies, waits for them, and re-layouts  18.1 us (2%)
  between operations  14.8 us (2%)
    psum x1, waiting for transfers between devices, shards(): lax.psum((*input_weight_grad, output_weight_grad, expand_weight_grad, red...  264 us
    psum x1, blocking collectives, shards(): lax.psum((*input_weight_grad, output_weight_grad, expand_weight_grad, red...  82.5 us
    dot_general x6, matrix products, dot_nt(): lax.dot_general(a, b, (((1,), (1,)), ((), ())), preferred_element_type=F32)  61.6 us
    pallas_call x1, Pallas kernels, attend_back(): pl.pallas_call(attend_back_kernel, grid=(pairs, rows // block), in_specs=...  60.3 us
    pallas_call x1, Pallas kernels, attend(): pl.pallas_call(attend_kernel, grid=(pairs, rows // block), in_specs=[tile...  48.8 us
    dot_general x6, matrix products, dot_tn(): lax.dot_general(a, b, (((0,), (0,)), ((), ())), preferred_element_type=F32)  37.9 us
    dot_general x6, matrix products, dot_nn(): lax.dot_general(a, b, (((1,), (0,)), ((), ())), preferred_element_type=F32)  32.1 us
    all_gather x4, waiting for transfers between devices, gather(): return lax.all_gather(values, 'tensor', axis=0, tiled=True)  27 us
  transfers between devices with their start and end apart: 9, of which 5 were waited for; matrix products, arithmetic and copies ran while one was open for 12% of the time, Pallas kernels for 0%

profile of v1, /device:TPU:0, one launch (start us, length us, event | category | flops | bytes accessed | tf_op | source)
XLA Modules:
  0.0 742.5 jit_solution(9705197737704748410)
XLA Ops:
  7.3 2.6 convert_reduce_fusion.2
  10.2 1.0 multiply_reduce_fusion
  11.3 1.5 add_convert_fusion.2
  12.8 0.4 copy-done.23
  13.2 3.1 convolution_convert_fusion.6.k_ref
  16.2 3.0 add_convert_fusion.6.v_ref
  19.3 3.0 add_convert_fusion.7.q_ref
  22.3 48.8 %attend.1 = (bf16[1568,512]{1,0:T(8,128)(2,1)}, f32[1568,512]{1,0:T(8,128)}, bf16[8,1568,1568]{2,1,0:T(8,128)(2,1)}) custom-call(bf16[1568,512]{1,0:T(8,128)(2,1)} %add_convert_fusion.7.q_ref, bf16[1568,512]{1,0:T(8,128)(2,1)} %convolution_convert_fusion.6.k_ref, bf16[1568,512]{1,0:T(8,128)(2,1)} %add_convert_fusion.6.v_ref), custom_call_target="tpu_custom_call" | custom-call | flops 20141047808 | bytes 39337984 | tf_op jit(solution)/shard_map/attend/pallas_call | solution.py:66
  71.2 4.9 convolution_convert_fusion.4
  76.4 5.4 convert_element_type.109
  81.8 8.4 %reduce-scatter.5.cloned.1.call-done = bf16[784,1024]{1,0:T(8,128)(2,1)} async-done(((bf16[1568,1024]{1,0:T(8,128)(2,1)}), bf16[784,1024]{1,0:T(8,128)(2,1)}) %reduce-scatter.5.cloned.1.call-update) | async-done | bytes 1605648 | tf_op jit(solution)/shard_map/reduce_scatter | solution.py:168
  90.3 3.6 fusion.26
  93.9 0.5 multiply_reduce_fusion.2
  94.4 0.6 copy-done.33
  95.0 0.6 copy-done.1
  95.6 0.6 copy-done.29
  96.2 1.7 add_convert_fusion.5
  98.0 13.6 %all-gather.5.cloned.1.call-done = bf16[1568,1024]{1,0:T(8,128)(2,1)} async-done(((bf16[784,1024]{1,0:T(8,128)(2,1)}), bf16[1568,1024]{1,0:T(8,128)(2,1)}) %all-gather.5.cloned.1.call-update) | async-done | bytes 3211280 | tf_op jit(solution)/shard_map/all_gather | solution.py:171
  111.6 9.9 %fusion.29 = f32[1568,2048]{1,0:T(8,128)S(1)} fusion(bf16[1568,1024]{1,0:T(8,128)(2,1)} %all-gather.5.cloned.1.call-done, bf16[1024,2048]{1,0:T(8,128)(2,1)} %param.25), kind=kOutput, calls=%fused_computation.93 | convolution fusion | flops 6576668672 | bytes 20250624 | tf_op jit(solution)/shard_map/dot_general | solution.py:31
  121.5 38.7 %fusion.23 = (bf16[2048]{0:T(1024)(128)(2,1)}, bf16[1568,2048]{1,0:T(8,128)(2,1)S(1)}, f32[1568,2048]{1,0:T(8,128)}) fusion(f32[1568,2048]{1,0:T(8,128)S(1)} %fusion.29, f32[2048]{0:T(1024)S(1)} %copy-done.36, bf16[1568,1024]{1,0:T(8,128)(2,1)S(1)} %copy-done.6, bf16[2048,1024]{1,0:T(8,128)(2,1)S(1)} %copy-done.43), kind=kOutput, calls=%fused_computation.88 | convolution fusion | flops 6814300160 | bytes 39530496 | tf_op jit(solution)/shard_map/dot_general | solution.py:35
  160.3 2.7 copy-done.50
  163.0 8.4 %convolution_convert_fusion.2 = bf16[1568,1024]{1,0:T(8,128)(2,1)} fusion(bf16[1568,2048]{1,0:T(8,128)(2,1)S(1)} %get-tuple-element.42, bf16[1024,2048]{1,0:T(8,128)(2,1)S(1)} %copy-done.42), kind=kOutput, calls=%fused_computation.36 | convolution fusion | flops 6578274304 | bytes 13828096 | tf_op jit(solution)/shard_map/dot_general | solution.py:35
  171.5 0.4 reduce-scatter.7.cloned.1.call-start
  171.9 10.9 %multiply_convert_fusion = bf16[1568,2048]{1,0:T(8,128)(2,1)S(1)} fusion(f32[1568,2048]{1,0:T(8,128)} %get-tuple-element.43, f32[1568,2048]{1,0:T(8,128)} %copy-done.9, f32[2048]{0:T(1024)S(1)} %copy-done.36), kind=kLoop, calls=%fused_computation.3 | loop fusion | flops 12845056 | bytes 32120832 | tf_op jit(solution)/shard_map/convert_element_type | solution.py:186
  182.9 2.8 copy-done.12
  185.6 8.2 %convolution_convert_fusion.3 = bf16[1568,1024]{1,0:T(8,128)(2,1)} fusion(bf16[1568,2048]{1,0:T(8,128)(2,1)S(1)} %multiply_convert_fusion, bf16[2048,1024]{1,0:T(8,128)(2,1)S(1)} %copy-done.44), kind=kOutput, calls=%fused_computation.37 | convolution fusion | flops 6578274304 | bytes 13828096 | tf_op jit(solution)/shard_map/dot_general | solution.py:31
  193.9 0.6 copy-done.26
  194.5 3.7 fusion.12
  198.3 8.2 %reduce-scatter.7.cloned.1.call-done = bf16[784,1024]{1,0:T(8,128)(2,1)} async-done(((bf16[1568,1024]{1,0:T(8,128)(2,1)}), bf16[784,1024]{1,0:T(8,128)(2,1)}) %reduce-scatter.7.cloned.1.call-update) | async-done | bytes 1605648 | tf_op jit(solution)/shard_map/reduce_scatter | solution.py:168
  206.4 5.1 fusion.25
  211.5 1.7 copy-done.3
  213.2 1.6 fusion.14
  215.1 13.4 %all-gather.9.cloned.1.call-done = bf16[1568,1024]{1,0:T(8,128)(2,1)} async-done(((bf16[784,1024]{1,0:T(8,128)(2,1)}), bf16[1568,1024]{1,0:T(8,128)(2,1)}) %all-gather.9.cloned.1.call-update) | async-done | bytes 3211280 | tf_op jit(solution)/shard_map/all_gather | solution.py:171
  228.5 4.9 convolution_convert_fusion.5.g_ref
  233.4 60.3 %attend_back.1 = (bf16[1568,512]{1,0:T(8,128)(2,1)}, bf16[1568,512]{1,0:T(8,128)(2,1)}, bf16[1568,512]{1,0:T(8,128)(2,1)}) custom-call(bf16[1568,512]{1,0:T(8,128)(2,1)} %add_convert_fusion.7.q_ref, bf16[1568,512]{1,0:T(8,128)(2,1)} %convolution_convert_fusion.6.k_ref, bf16[1568,512]{1,0:T(8,128)(2,1)} %add_convert_fusion.6.v_ref, ...), custom_call_target="tpu_custom_call" | custom-call | flops 40282095616 | bytes 39337984 | tf_op jit(solution)/shard_map/attend_back/pallas_call | solution.py:125
  293.8 3.8 fusion.18
  297.6 1.9 fusion.19
  299.5 3.8 add_convert_fusion.1
  303.4 0.6 copy-done.35
  304.3 12.8 %convolution_convert_fusion = bf16[2048,1024]{1,0:T(8,128)(2,1)} fusion(bf16[1568,2048]{1,0:T(8,128)(2,1)} %copy-done.12, bf16[1568,1024]{1,0:T(8,128)(2,1)} %param.29), kind=kOutput, calls=%fused_computation.34 | convolution fusion | flops 6578765824 | bytes 13828096 | tf_op jit(solution)/shard_map/dot_general | solution.py:39
  317.1 3.7 multiply_reduce_fusion.1
  320.9 3.7 fusion.13
  324.7 4.0 add_convert_fusion.3
  329.1 12.8 %convolution_convert_fusion.1 = bf16[1024,2048]{1,0:T(8,128)(2,1)} fusion(bf16[1568,1024]{1,0:T(8,128)(2,1)} %all-gather.5.cloned.1.call-done, bf16[1568,2048]{1,0:T(8,128)(2,1)} %copy-done.50), kind=kOutput, calls=%fused_computation.35 | convolution fusion | flops 6578765824 | bytes 13828096 | tf_op jit(solution)/shard_map/dot_general | solution.py:39
  341.9 3.1 fusion.16
  345.0 3.1 fusion.15
  348.0 3.1 fusion.17
  351.1 3.1 convolution_convert_fusion.7
  354.2 2.5 reduce
  356.7 1.7 reduce.2
  358.7 2.5 reduce.1
  361.3 3.4 psum.56
  365.1 82.5 %psum.57 = bf16[9216]{0:T(1024)(128)(2,1)S(1)} all-reduce(bf16[9216]{0:T(1024)(128)(2,1)S(1)} %constant_dynamic-update-slice_fusion), channel_id=1, replica_groups=mesh['dp'=16,'tensor'=2] {'dp'}, use_global_device_ids=true, to_apply=%region_24.0 | all-reduce | flops 9216 | bytes 36864 | tf_op jit(solution)/shard_map/psum | solution.py:227
  447.7 0.6 slice.70
  448.3 0.6 fusion.28
  448.9 0.6 fusion.27
  449.5 264.0 %all-reduce.3.cloned.1.call-done = (bf16[1,1024,512]{2,1,0:T(8,128)(2,1)}, bf16[1,1024,512]{2,1,0:T(8,128)(2,1)}, bf16[1,1024,512]{2,1,0:T(8,128)(2,1)}, bf16[51...) async-done(((bf16[1,1024,512]{2,1,0:T(8,128)(2,1)}, bf16[1,1024,512]{2,1,0:T(8,128)(2,1)}, bf16[1,1024,512]{2,1,0:T(8,128)(2,1)}, ...) | async-done | bytes 12582928 | tf_op jit(solution)/shard_map/psum | solution.py:227
  713.5 2.8 convert_element_type.139
  716.2 6.8 convert_element_type.141
  723.1 4.4 convert_element_type.143
  727.5 3.2 convert_bitcast_fusion
  730.7 1.7 copy.45
  732.4 1.4 copy-done.18
  733.8 1.7 copy.46
  (130 shorter events, 2.9 us)
Async XLA Ops:
  7.2 64.0 %copy-start = (bf16[512,1024]{1,0:T(8,128)(2,1)S(1)}, bf16[512,1024]{1,0:T(8,128)(2,1)}, u32[]{:S(2)}) copy-start(bf16[512,1024]{1,0:T(8,128)(2,1)} %param.21) | copy-start | bytes 3145732
  7.2 4.0 copy-start.27
  7.2 4.0 copy-start.37
  7.2 83.0 %reduce-scatter.5.cloned.1.call-start = ((), (), s32[]{:S(2)}) async-start(), calls=%async_computation.4 | async-start | bytes 4816896 | tf_op jit(solution)/shard_map/reduce_scatter | solution.py:168
  7.3 3.0 copy-start.2
  11.3 1.9 copy-start.23
  12.8 6.5 copy-start.14
  13.1 3.1 copy-start.45
  16.2 3.0 copy-start.46
  76.1 35.5 %all-gather.5.cloned.1.call-start = ((), (), s32[]{:S(2)}) async-start(), calls=%async_computation.5 | async-start | bytes 4816896 | tf_op jit(solution)/shard_map/all_gather | solution.py:171
  76.4 13.9 %copy-start.38 = (f32[1024]{0:T(1024)S(1)}, f32[1024]{0:T(1024)}, u32[]{:S(2)}) copy-start(f32[1024]{0:T(1024)} %param.22) | copy-start | bytes 12292
  93.9 1.7 copy-start.1
  93.9 2.3 copy-start.31
  93.9 2.3 copy-start.39
  93.9 1.7 copy-start.25
  94.4 0.6 copy-start.33
  95.6 0.6 copy-start.29
  97.9 23.5 %copy-start.36 = (f32[2048]{0:T(1024)S(1)}, f32[2048]{0:T(1024)}, u32[]{:S(2)}) copy-start(f32[2048]{0:T(1024)} %param.26) | copy-start | bytes 24580
  97.9 96.0 %reduce-scatter.9.cloned.1.call-start = ((), (), s32[]{:S(2)}) async-start(), calls=%async_computation.8 | async-start | bytes 4816896 | tf_op jit(solution)/shard_map/reduce_scatter | solution.py:168
  111.6 9.9 %copy-start.6 = (bf16[1568,1024]{1,0:T(8,128)(2,1)S(1)}, bf16[1568,1024]{1,0:T(8,128)(2,1)}, u32[]{:S(2)}) copy-start(bf16[1568,1024]{1,0:T(8,128)(2,1)} %param.29) | copy-start | bytes 9633796
  111.6 9.9 %copy-start.43 = (bf16[2048,1024]{1,0:T(8,128)(2,1)S(1)}, bf16[2048,1024]{1,0:T(8,128)(2,1)}, u32[]{:S(2)}) copy-start(bf16[2048,1024]{1,0:T(8,128)(2,1)} %param.27) | copy-start | bytes 12582916
  121.5 38.8 %copy-start.9 = (f32[1568,2048]{1,0:T(8,128)}, f32[1568,2048]{1,0:T(8,128)S(1)}, u32[]{:S(2)}) copy-start(f32[1568,2048]{1,0:T(8,128)S(1)} %fusion.29) | copy-start | bytes 38535172
  121.5 41.5 %copy-start.42 = (bf16[1024,2048]{1,0:T(8,128)(2,1)S(1)}, bf16[1024,2048]{1,0:T(8,128)(2,1)}, u32[]{:S(2)}) copy-start(bf16[1024,2048]{1,0:T(8,128)(2,1)} %param.25) | copy-start | bytes 12582916
  160.3 2.7 copy-start.50
  171.5 34.9 %reduce-scatter.7.cloned.1.call-start = ((), (), s32[]{:S(2)}) async-start(), calls=%async_computation.6 | async-start | bytes 4816896 | tf_op jit(solution)/shard_map/reduce_scatter | solution.py:168
  171.9 13.7 %copy-start.44 = (bf16[2048,1024]{1,0:T(8,128)(2,1)S(1)}, bf16[2048,1024]{1,0:T(8,128)(2,1)}, u32[]{:S(2)}) copy-start(bf16[2048,1024]{1,0:T(8,128)(2,1)} %param.27) | copy-start | bytes 12582916
  182.9 2.8 copy-start.12
  193.8 0.7 copy-start.26
  193.8 0.7 copy-start.30
  193.8 0.7 copy-start.32
  193.8 4.4 copy-start.34
  193.8 12.6 %copy-start.40 = (f32[1024]{0:T(1024)S(1)}, f32[1024]{0:T(1024)}, u32[]{:S(2)}) copy-start(f32[1024]{0:T(1024)} %param.28) | copy-start | bytes 12292
  193.9 34.6 %all-gather.9.cloned.1.call-start = ((), (), s32[]{:S(2)}) async-start(), calls=%async_computation.9 | async-start | bytes 4816896 | tf_op jit(solution)/shard_map/all_gather | solution.py:171
  194.5 11.9 %copy-start.11 = (bf16[784,1024]{1,0:T(8,128)(2,1)S(1)}, bf16[784,1024]{1,0:T(8,128)(2,1)}, u32[]{:S(2)}) copy-start(bf16[784,1024]{1,0:T(8,128)(2,1)} %reduce-scatter.9.cloned.1.call-done) | copy-start | bytes 4816900
  206.4 6.8 copy-start.7
  211.5 1.7 copy-start.3
  214.8 102.3 %reduce-scatter.11.cloned.1.call-start = ((), (), s32[]{:S(2)}) async-start(), calls=%async_computation.10 | async-start | bytes 4816896 | tf_op jit(solution)/shard_map/reduce_scatter | solution.py:168
  293.8 3.8 copy-start.24
  293.8 3.8 copy-start.47
  297.6 1.9 copy-start.10
  303.3 0.7 copy-start.35
  303.3 57.9 %all-gather.7.cloned.1.call-start = ((), (), s32[]{:S(2)}) async-start(), calls=%async_computation.7 | async-start | bytes 4816896 | tf_op jit(solution)/shard_map/all_gather | solution.py:171
  304.1 13.1 %copy-start.28 = (f32[1024]{0:T(1024)S(1)}, f32[1024]{0:T(1024)}, u32[]{:S(2)}) copy-start(f32[1024]{0:T(1024)} %param.16) | copy-start | bytes 12292
  304.1 145.4 %all-gather.11.cloned.1.call-start = ((), (), s32[]{:S(2)}) async-start(), calls=%async_computation.11 | async-start | bytes 4816896 | tf_op jit(solution)/shard_map/all_gather | solution.py:171
  317.1 3.8 copy-start.5
  317.1 7.5 %copy-start.8 = (bf16[1568,1024]{1,0:T(8,128)(2,1)S(1)}, bf16[1568,1024]{1,0:T(8,128)(2,1)}, u32[]{:S(2)}) copy-start(bf16[1568,1024]{1,0:T(8,128)(2,1)} %param.29) | copy-start | bytes 9633796
  320.9 3.8 copy-start.4
  328.7 384.7 %all-reduce.3.cloned.1.call-start = ((), (), s32[]{:S(2)}) async-start(), calls=%async_computation.12 | async-start | bytes 25165824 | tf_op jit(solution)/shard_map/psum | solution.py:227
  329.0 12.9 %copy-start.15 = (bf16[1568,1024]{1,0:T(8,128)(2,1)S(1)}, bf16[1568,1024]{1,0:T(8,128)(2,1)}, u32[]{:S(2)}) copy-start(bf16[1568,1024]{1,0:T(8,128)(2,1)} %copy-done.14) | copy-start | bytes 9633796
  329.1 12.8 %copy-start.48 = (bf16[1568,512]{1,0:T(8,128)(2,1)S(1)}, bf16[1568,512]{1,0:T(8,128)(2,1)}, u32[]{:S(2)}) copy-start(bf16[1568,512]{1,0:T(8,128)(2,1)} %get-tuple-element.25) | copy-start | bytes 4816900
  341.9 3.1 copy-start.19
  348.0 3.1 copy-start.17
  348.0 3.1 copy-start.49
  356.7 8.4 %copy-start.41 = (bf16[2048]{0:T(1024)(128)(2,1)S(1)}, bf16[2048]{0:T(1024)(128)(2,1)}, u32[]{:S(2)}) copy-start(bf16[2048]{0:T(1024)(128)(2,1)} %get-tuple-element.41) | copy-start | bytes 12292
  716.2 6.8 copy-start.13
  723.1 4.5 copy-start.20
  723.1 4.5 copy-start.21
  723.1 4.5 copy-start.22
  727.5 3.2 copy-start.16
  730.7 3.1 copy-start.18
Sparse Core Ops, SparseCore 0:
  76.2 13.9 reduce-scatter.4
  98.1 13.4 all-gather.4
  171.6 12.4 reduce-scatter.8
  193.9 12.4 reduce-scatter.6
  215.0 13.4 all-gather.8
  303.4 12.4 reduce-scatter.10
  317.4 13.4 all-gather.6
  333.1 13.3 all-gather.10
  354.3 359.0 all-reduce.2

commit v2 on v1

--- a/solution.py
+++ b/solution.py
@@ -39,7 +39,7 @@
     return lax.dot_general(a, b, (((0,), (0,)), ((), ())), preferred_element_type=F32)
 
 
-def attend_kernel(q_ref, k_ref, v_ref, out_ref, inverse_ref, weights_ref):
+def attend_kernel(q_ref, k_ref, v_ref, out_ref, exact_ref, inverse_ref, weights_ref):
     low_half = lax.broadcasted_iota(jnp.int32, (1, PAIR), 1) < HEAD_DIM
     zero = jnp.zeros((), BF16)
     keys, values, queries = k_ref[...], v_ref[...], q_ref[...]
@@ -54,7 +54,9 @@
         weights_ref[head] = weights
         mixed.append(dot_nn(weights, values) * inverse)
         inverses.append(inverse)
-    out_ref[...] = jnp.where(low_half, mixed[0], mixed[1]).astype(BF16)
+    exact = jnp.where(low_half, mixed[0], mixed[1])
+    out_ref[...] = exact.astype(BF16)
+    exact_ref[...] = exact
     inverse_ref[...] = jnp.where(low_half, inverses[0], inverses[1])
 
 
@@ -67,9 +69,10 @@
         attend_kernel,
         grid=(pairs, rows // block),
         in_specs=[tile, whole, whole],
-        out_specs=[tile, tile, pl.BlockSpec((2, block, rows), lambda p, i: (p, i, 0))],
+        out_specs=[tile, tile, tile, pl.BlockSpec((2, block, rows), lambda p, i: (p, i, 0))],
         out_shape=[
             jax.ShapeDtypeStruct((rows, width), BF16),
+            jax.ShapeDtypeStruct((rows, width), F32),
             jax.ShapeDtypeStruct((rows, width), F32),
             jax.ShapeDtypeStruct((2 * pairs, rows, rows), BF16),
         ],
@@ -83,12 +86,171 @@
     )(queries, keys, values)
 
 
-def attend_back_kernel(
-    q_ref, k_ref, v_ref, g_ref, o_ref, inverse_ref, weights_ref, dq_ref, dk_ref, dv_ref, dk_sum, dv_sum
-):
+def orders_of(bits):
+    if bits == 4:
+        return ((0, 1, 2, 3), (1, 0, 2, 3), (2, 0, 1, 3), (2, 1, 0, 3))
+    return tuple(tuple((i + j) % bits for j in range(bits)) for i in (0, 1, 2, 3))
+
+
+class Part:
+    def __init__(self, array, first, each, cols, dtype, order):
+        self.array, self.first, self.each = array, first, each
+        self.cols, self.dtype, self.order = cols, dtype, order
+
+
+def parts_of(array, shape, dtype, n, shares, orders):
+    unit = 16 if dtype == BF16 else 8
+    units = shape[0] // (n * unit)
+    counts = [units * share // sum(shares) for share in shares]
+    counts[0] += units - sum(counts)
+    parts, first = [], 0
+    for count, order in zip(counts, orders):
+        if count:
+            parts.append(Part(array, first, count * unit, shape[1], dtype, order))
+            first += n * count * unit
+    return parts
+
+
+def divides(shape, dtype, n):
+    return shape[0] % (n * (16 if dtype == BF16 else 8)) == 0
+
+
+class Reduction:
+    def __init__(self, parts, n, bufs, lands, gathers, sems):
+        self.parts, self.n, self.bits = parts, n, n.bit_length() - 1
+        self.bufs, self.lands, self.gathers = bufs, lands, gathers
+        self.load_sem, self.store_sem, self.send_sem, self.recv_sem = sems
+        me = lax.axis_index("dp")
+        self.digit = [(me // (1 << b)) % 2 for b in range(self.bits)]
+        self.partner = [me + (1 << b) * (1 - 2 * self.digit[b]) for b in range(self.bits)]
+
+    def greet(self):
+        barrier = pltpu.get_barrier_semaphore()
+        for b in range(self.bits):
+            pl.semaphore_signal(
+                barrier, inc=1, device_id={"dp": self.partner[b]}, device_id_type=pl.DeviceIdType.MESH
+            )
+        pl.semaphore_wait(barrier, self.bits)
+
+    def rows(self, i, position):
+        part, shard = self.parts[i], 0
+        for level, b in enumerate(part.order):
+            flip = (position >> (self.bits - 1 - level)) & 1
+            shard = shard + (1 << b) * ((1 - self.digit[b]) if flip else self.digit[b])
+        return pl.ds(pl.multiple_of(part.first + shard * part.each, 8), part.each)
+
+    def load(self, i, ref):
+        for position in range(self.n):
+            pltpu.make_async_copy(ref.at[self.rows(i, position), :], self.bufs[i].at[position], self.load_sem.at[i]).start()
+
+    def load_wait(self, i):
+        pltpu.make_async_copy(self.bufs[i], self.bufs[i], self.load_sem.at[i]).wait()
+
+    def store(self, i, ref):
+        for position in range(self.n):
+            pltpu.make_async_copy(self.gathers[i].at[position], ref.at[self.rows(i, position), :], self.store_sem.at[i]).start()
+
+    def store_wait(self, i):
+        pltpu.make_async_copy(self.gathers[i], self.gathers[i], self.store_sem.at[i]).wait()
+
+    def load_own(self, i, ref):
+        pltpu.make_async_copy(ref, self.gathers[i].at[0], self.load_sem.at[i]).start()
+
+    def load_own_wait(self, i):
+        pltpu.make_async_copy(self.gathers[i].at[0], self.gathers[i].at[0], self.load_sem.at[i]).wait()
+
+    def store_own(self, i, ref):
+        pltpu.make_async_copy(self.gathers[i].at[0], ref, self.store_sem.at[i]).start()
+
+    def store_own_wait(self, i):
+        pltpu.make_async_copy(self.gathers[i].at[0], self.gathers[i].at[0], self.store_sem.at[i]).wait()
+
+    def exchange(self, i, number):
+        level = number if number < self.bits else 2 * self.bits - 1 - number
+        half = self.n >> (level + 1)
+        if number < self.bits:
+            source, target = self.bufs[i].at[pl.ds(half, half)], self.lands[i].at[pl.ds(self.n - 2 * half, half)]
+        else:
+            source, target = self.gathers[i].at[pl.ds(0, half)], self.gathers[i].at[pl.ds(half, half)]
+        k = i * 2 * self.bits + number
+        return pltpu.make_async_remote_copy(
+            source,
+            target,
+            self.send_sem.at[k],
+            self.recv_sem.at[k],
+            device_id={"dp": self.partner[self.parts[i].order[level]]},
+            device_id_type=pl.DeviceIdType.MESH,
+        )
+
+    def finish(self, i, number):
+        self.exchange(i, number).wait()
+        if number < self.bits:
+            half = self.n >> (number + 1)
+            start = self.n - 2 * half
+            buf, land = self.bufs[i], self.lands[i]
+            to = self.gathers[i] if number == self.bits - 1 else buf
+
+            def add(j, carry):
+                to[j] = (buf[j].astype(F32) + land[start + j].astype(F32)).astype(buf.dtype)
+                return carry
+
+            lax.fori_loop(0, half, add, 0)
+
+
+def buffers(summed, gathered, n):
+    parts, bits, count = gathered, n.bit_length() - 1, len(gathered)
+    return (
+        [pltpu.VMEM((n, p.each, p.cols), p.dtype) for p in summed]
+        + [pltpu.VMEM((n - 1, p.each, p.cols), p.dtype) for p in summed]
+        + [pltpu.VMEM((n, p.each, p.cols), p.dtype) for p in gathered]
+        + [pltpu.SemaphoreType.DMA((count,))] * 2
+        + [pltpu.SemaphoreType.DMA((count * 2 * bits,))] * 2
+    )
+
+
+def attend_back_kernel(parts, n, arrays, total, *refs):
+    q_ref, k_ref, v_ref, g_ref, o_ref, inverse_ref, weights_ref = refs[:7]
+    sources, refs = refs[7 : 7 + arrays], refs[7 + arrays :]
+    dq_ref, dk_ref, dv_ref = refs[:3]
+    owns, refs = refs[3 : 3 + len(parts)], refs[3 + len(parts) :]
+    dk_sum, dv_sum = refs[:2]
+    refs = refs[2:]
+    count = len(parts)
+    sums = Reduction(parts, n, refs[:count], refs[count : 2 * count], refs[:count], refs[2 * count :])
     step, steps = pl.program_id(1), pl.num_programs(1)
     low_half = lax.broadcasted_iota(jnp.int32, (1, PAIR), 1) < HEAD_DIM
     zero = jnp.zeros((), BF16)
+    now = pl.program_id(0) * steps + step
+
+    @pl.when(now == 0)
+    def _():
+        sums.greet()
+        for i in range(count):
+            sums.load(i, sources[parts[i].array])
+        for i in range(count):
+            sums.load_wait(i)
+            sums.exchange(i, 0).start()
+
+    def advance(i, number):
+        sums.finish(i, number)
+        if number + 1 < sums.bits:
+            sums.exchange(i, number + 1).start()
+        else:
+            sums.store_own(i, owns[i])
+
+    events = [(i, number) for number in range(sums.bits) for i in range(count)]
+    slots = []
+    for i, number in events:
+        first, last = EVENT_TIMES[min(number, 3)]
+        slots.append(min(total, int((first + (last - first) * i / max(count - 1, 1)) * total)))
+    for slot in sorted(set(slots)):
+        if slot < total:
+
+            @pl.when(now == slot)
+            def _(slot=slot):
+                for event, place in zip(events, slots):
+                    if place == slot:
+                        advance(*event)
 
     @pl.when(step == 0)
     def _():
@@ -97,7 +259,7 @@
 
     keys, values, queries = k_ref[...], v_ref[...], q_ref[...]
     grads = (g_ref[...].astype(F32) * inverse_ref[...]).astype(BF16)
-    products = grads.astype(F32) * o_ref[...].astype(F32)
+    products = grads.astype(F32) * o_ref[...]
     query_grad = None
     for head in range(2):
         own = low_half if head == 0 else ~low_half
@@ -116,27 +278,99 @@
         dk_ref[...] = (dk_sum[...] * 0.125).astype(BF16)
         dv_ref[...] = dv_sum[...].astype(BF16)
 
-
-def attend_back(queries, keys, values, grads, outs, inverse, weights, block=224):
+    @pl.when(now == total - 1)
+    def _():
+        for event, place in zip(events, slots):
+            if place == total:
+                advance(*event)
+        for i in range(count):
+            sums.store_own_wait(i)
+
+
+def attend_back(queries, keys, values, grads, outs, inverse, weights, sources, parts, n, block=224):
     rows, width = queries.shape
     pairs = width // PAIR
     tile = pl.BlockSpec((block, PAIR), lambda p, i: (i, p))
     whole = pl.BlockSpec((rows, PAIR), lambda p, i: (0, p))
-    return pl.pallas_call(
-        attend_back_kernel,
+    anywhere = pl.BlockSpec(memory_space=pl.ANY)
+    results = pl.pallas_call(
+        functools.partial(attend_back_kernel, parts, n, len(sources), pairs * (rows // block)),
         grid=(pairs, rows // block),
-        in_specs=[tile, whole, whole, tile, tile, tile, pl.BlockSpec((2, block, rows), lambda p, i: (p, i, 0))],
-        out_specs=[tile, whole, whole],
-        out_shape=[jax.ShapeDtypeStruct((rows, width), BF16)] * 3,
-        scratch_shapes=[pltpu.VMEM((rows, PAIR), F32)] * 2,
-        compiler_params=pltpu.CompilerParams(vmem_limit_bytes=60 << 20),
+        in_specs=[tile, whole, whole, tile, tile, tile, pl.BlockSpec((2, block, rows), lambda p, i: (p, i, 0))]
+        + [anywhere] * len(sources),
+        out_specs=[tile, whole, whole] + [anywhere] * len(parts),
+        out_shape=[jax.ShapeDtypeStruct((rows, width), BF16)] * 3
+        + [jax.ShapeDtypeStruct((p.each, p.cols), p.dtype) for p in parts],
+        scratch_shapes=[pltpu.VMEM((rows, PAIR), F32)] * 2 + buffers(parts, [], n)[: 2 * len(parts)] + buffers([], parts, n)[len(parts) :],
+        compiler_params=pltpu.CompilerParams(vmem_limit_bytes=60 << 20, collective_id=0, has_side_effects=True),
         cost_estimate=pl.CostEstimate(
             flops=16 * pairs * rows * rows * HEAD_DIM * 4,
             bytes_accessed=4 * pairs * rows * rows,
             transcendentals=0,
         ),
         name="attend_back",
-    )(queries, keys, values, grads, outs, inverse, weights)
+    )(queries, keys, values, grads, outs, inverse, weights, *sources)
+    return results[:3], results[3:]
+
+
+def spread_kernel(own_parts, full_parts, n, own_arrays, full_arrays, *refs):
+    owns, refs = refs[: len(own_parts)], refs[len(own_parts) :]
+    sources, refs = refs[:full_arrays], refs[full_arrays:]
+    spread, refs = refs[:own_arrays], refs[own_arrays:]
+    summed, refs = refs[:full_arrays], refs[full_arrays:]
+    parts = own_parts + full_parts
+    count, skip = len(parts), len(own_parts)
+    full = len(full_parts)
+    bufs, lands, gathers = refs[:full], refs[full : 2 * full], refs[2 * full : 2 * full + count]
+    none = (None,) * skip
+    sums = Reduction(parts, n, none + bufs, none + lands, gathers, refs[2 * full + count :])
+    last = 2 * sums.bits
+    sums.greet()
+    for i in range(skip):
+        sums.load_own(i, owns[i])
+    for i in range(skip, count):
+        sums.load(i, sources[parts[i].array])
+
+    def step(i, number):
+        if i < skip and number == sums.bits:
+            sums.load_own_wait(i)
+        elif number == 0:
+            sums.load_wait(i)
+        else:
+            sums.finish(i, number - 1)
+        if number < last:
+            sums.exchange(i, number).start()
+        else:
+            sums.store(i, (spread if i < skip else summed)[parts[i].array])
+
+    for turn in range(last + 2):
+        if turn <= last:
+            for i in range(skip, count):
+                step(i, turn)
+        number = turn - 1
+        if sums.bits <= number <= last:
+            for i in range(skip):
+                step(i, number)
+    for i in range(count):
+        sums.store_wait(i)
+
+
+def spread_and_sum(owns, own_parts, own_shapes, sources, full_parts, n):
+    anywhere = pl.BlockSpec(memory_space=pl.ANY)
+    shapes = list(own_shapes) + [jax.ShapeDtypeStruct(s.shape, s.dtype) for s in sources]
+    results = pl.pallas_call(
+        functools.partial(spread_kernel, own_parts, full_parts, n, len(own_shapes), len(sources)),
+        in_specs=[anywhere] * (len(owns) + len(sources)),
+        out_specs=[anywhere] * len(shapes),
+        out_shape=shapes,
+        scratch_shapes=buffers(full_parts, own_parts + full_parts, n),
+        compiler_params=pltpu.CompilerParams(vmem_limit_bytes=60 << 20, collective_id=1, has_side_effects=True),
+        name="spread_and_sum",
+    )(*owns, *sources)
+    return results[: len(own_shapes)], results[len(own_shapes) :]
+
+
+EVENT_TIMES = ((0.3, 0.58), (0.62, 0.88), (0.9, 1.0), (1.0, 1.0))
 
 
 def column_sum(values):
@@ -177,7 +411,7 @@
     queries = (dot_nn(normed, stacked_weight[0]) + query_bias).astype(BF16)
     keys = dot_nn(normed, stacked_weight[1]).astype(BF16)
     values = (dot_nn(normed, stacked_weight[2]) + value_bias).astype(BF16)
-    attended, inverse, weights = attend(queries, keys, values)
+    attended, exact, inverse, weights = attend(queries, keys, values)
     own_inputs = lax.dynamic_slice_in_dim(inputs, first_row, share, 0)
     middle = own_inputs + scatter(dot_nn(attended, output_weight).astype(BF16)).astype(F32) + output_bias
     normed_two = layer_norm(middle, feedforward_gain, feedforward_shift).astype(BF16)
@@ -202,7 +436,15 @@
     output_bias_grad = column_sum(branch_grad)
     output_weight_grad = dot_tn(attended, branch_grad).astype(BF16)
     attended_grad = dot_nt(branch_grad, output_weight).astype(BF16)
-    joint_grad = attend_back(queries, keys, values, attended_grad, attended, inverse, weights)
+    n = lax.axis_size("dp")
+    orders = orders_of(n.bit_length() - 1)
+    feed = (reduce_weight_grad, expand_weight_grad)
+    feed_parts = parts_of(0, feed[0].shape, BF16, n, (3, 3, 2), orders[:3]) + parts_of(
+        1, feed[1].shape, BF16, n, (1, 1, 2), (orders[0], orders[1], orders[3])
+    )
+    joint_grad, owns = attend_back(
+        queries, keys, values, attended_grad, exact, inverse, weights, feed, feed_parts, n
+    )
     query_bias_grad = column_sum(joint_grad[0])
     value_bias_grad = column_sum(joint_grad[2])
     input_weight_grad = tuple(dot_tn(normed, part).astype(BF16) for part in joint_grad)
@@ -224,19 +466,23 @@
         expand_bias_grad,
     ]
     sizes = [part.shape[0] for part in small]
-    sums = lax.psum(
-        (
-            *input_weight_grad,
-            output_weight_grad,
-            expand_weight_grad,
-            reduce_weight_grad,
-            jnp.concatenate(small).astype(BF16),
-        ),
-        "dp",
-    )
-    sums = [part.astype(F32) for part in sums]
+    table_rows = -(-sum(sizes) // (n * 8 * 128)) * n * 8
+    table = jnp.pad(jnp.concatenate(small), (0, table_rows * 128 - sum(sizes))).reshape(table_rows, 128)
+    rest = [*input_weight_grad, output_weight_grad, table]
+    fits = [divides(part.shape, part.dtype, n) for part in rest]
+    sources, rest_parts = [], []
+    for which, part in enumerate(rest):
+        if fits[which]:
+            rest_parts += parts_of(len(sources), part.shape, part.dtype, n, (1,), (orders[which % 4],))
+            sources.append(part)
+    shapes = [jax.ShapeDtypeStruct(part.shape, part.dtype) for part in feed]
+    feed, summed = spread_and_sum(owns, feed_parts, shapes, sources, rest_parts, n)
+    summed = list(summed)
+    rest = [summed.pop(0) if fit else lax.psum(part, "dp") for part, fit in zip(rest, fits)]
+    sums = [part.astype(F32) for part in (*rest[:4], feed[1], feed[0])]
+    flat = rest[4].reshape(-1)
     ends = [sum(sizes[: i + 1]) for i in range(len(sizes))]
-    parts = [sums[6][end - size : end] for size, end in zip(sizes, ends)]
+    parts = [flat[end - size : end] for size, end in zip(sizes, ends)]
     norms = parts[0].reshape(4, -1)
     return (
         block_out,

time: 750 us -> 580 us (0.77)
  waiting for transfers between devices: 308 us -> 25.4 us
  Pallas kernels: 109 us -> 296 us
  blocking collectives: 85.9 us -> 3.45 us
    psum x1 -> x0, waiting for transfers between devices: 264 us -> none  [shards(): lax.psum((*input_weight_grad, output_weight_grad, expand_weight_grad, red...]
    pallas_call x1 -> x2, Pallas kernels: 60.3 us -> 246 us  [the longest x1 153 us: spread_and_sum(): pl.pallas_call(functools.partial(spread_kernel, own_parts, full_parts, n,...]
    psum x1 -> x0, blocking collectives: 82.5 us -> none  [shards(): lax.psum((*input_weight_grad, output_weight_grad, expand_weight_grad, red...]
    all_gather x4, waiting for transfers between devices: 27 us -> 13.7 us  [gather(): return lax.all_gather(values, 'tensor', axis=0, tiled=True)]
    convert_element_type x3 -> x4, other arithmetic: 14 us -> 18.2 us  [the longest x3 12.8 us: shards(): sums = [part.astype(F32) for part in (*rest[:4], feed[1], feed[0])]]
    unnamed x109 -> x110, local copies, waits for them, and re-layouts: 16.3 us -> 16 us
  transfers between devices with their start and end apart: 9 -> 8, of which waited for: 5 -> 4; matrix products, arithmetic and copies ran while one was open for 12% -> 20% of each run, Pallas kernels for 0% -> 27%
where the time goes in v2:
time: 580 us; the launch traced here: 572 us
  Pallas kernels  296 us (51%)
  matrix products  133 us (23%)
  other arithmetic  80.1 us (14%)
  waiting for transfers between devices  25.4 us (4%)
  local copies, waits for them, and re-layouts  18.4 us (3%)
  between operations  15.1 us (3%)
    pallas_call x1, Pallas kernels, spread_and_sum(): pl.pallas_call(functools.partial(spread_kernel, own_parts, full_parts, n,...  153 us
    pallas_call x1, Pallas kernels, attend_back(): pl.pallas_call(functools.partial(attend_back_kernel, parts, n, len(source...  93.8 us
    dot_general x6, matrix products, dot_nt(): lax.dot_general(a, b, (((1,), (1,)), ((), ())), preferred_element_type=F32)  61.6 us
    pallas_call x1, Pallas kernels, attend(): pl.pallas_call(attend_kernel, grid=(pairs, rows // block), in_specs=[tile...  49.2 us
    dot_general x6, matrix products, dot_tn(): lax.dot_general(a, b, (((0,), (0,)), ((), ())), preferred_element_type=F32)  39.6 us
    dot_general x6, matrix products, dot_nn(): lax.dot_general(a, b, (((1,), (0,)), ((), ())), preferred_element_type=F32)  32.2 us
    unnamed x110, local copies, waits for them, and re-layouts  16 us
    all_gather x4, waiting for transfers between devices, gather(): return lax.all_gather(values, 'tensor', axis=0, tiled=True)  13.7 us
  transfers between devices with their start and end apart: 8, of which 4 were waited for; matrix products, arithmetic and copies ran while one was open for 20% of the time, Pallas kernels for 27%

profile of v2, /device:TPU:0, one launch (start us, length us, event | category | flops | bytes accessed | tf_op | source)
XLA Modules:
  0.0 572.5 jit_solution(674588359033343616)
XLA Ops:
  7.3 2.6 convert_reduce_fusion.4
  9.8 0.4 copy-done.2
  10.2 1.0 multiply_reduce_fusion
  11.3 1.5 add_convert_fusion.2
  12.8 0.4 copy-done.23
  13.2 3.1 convolution_convert_fusion.6.k_ref.refs_1_
  16.2 3.0 add_convert_fusion.6.v_ref.refs_2_
  19.3 3.0 add_convert_fusion.7.q_ref.refs_0_
  22.3 49.2 %attend.1 = (bf16[1568,512]{1,0:T(8,128)(2,1)}, f32[1568,512]{1,0:T(8,128)}, f32[1568,512]{1,0:T(8,128)}, bf16[8,1568,1568]{2,1,0:T(8,128)(2,1)}) custom-call(bf16[1568,512]{1,0:T(8,128)(2,1)} %add_convert_fusion.7.q_ref.refs_0_, bf16[1568,512]{1,0:T(8,128)(2,1)} %convolution_convert_fusion.6.k_ref.refs_1_, bf16[1568,512]{1,0:T(8,128)(2,1)} %add_convert_fusion.6.v_ref.refs_2_), custom_call_target="tpu_custom_call" | custom-call | flops 20141047808 | bytes 39337984 | tf_op jit(solution)/shard_map/attend/pallas_call | solution.py:68
  71.5 4.9 convolution_convert_fusion.4
  76.5 0.3 all-gather.5.cloned.1.call-start
  76.8 5.4 convert_element_type.107
  82.2 8.4 %reduce-scatter.5.cloned.1.call-done = bf16[784,1024]{1,0:T(8,128)(2,1)} async-done(((bf16[1568,1024]{1,0:T(8,128)(2,1)}), bf16[784,1024]{1,0:T(8,128)(2,1)}) %reduce-scatter.5.cloned.1.call-update) | async-done | bytes 1605648 | tf_op jit(solution)/shard_map/reduce_scatter | solution.py:402
  90.6 3.6 fusion.22
  94.3 0.5 multiply_reduce_fusion.2
  94.8 0.6 copy-done.33
  95.4 0.5 copy-done.1
  95.9 0.6 copy-done.27
  96.5 1.7 add_convert_fusion.5
  98.3 13.6 %all-gather.5.cloned.1.call-done = bf16[1568,1024]{1,0:T(8,128)(2,1)} async-done(((bf16[784,1024]{1,0:T(8,128)(2,1)}), bf16[1568,1024]{1,0:T(8,128)(2,1)}) %all-gather.5.cloned.1.call-update) | async-done | bytes 3211280 | tf_op jit(solution)/shard_map/all_gather | solution.py:405
  111.9 9.9 %fusion.23 = f32[1568,2048]{1,0:T(8,128)S(1)} fusion(bf16[1568,1024]{1,0:T(8,128)(2,1)} %all-gather.5.cloned.1.call-done, bf16[1024,2048]{1,0:T(8,128)(2,1)} %param.25), kind=kOutput, calls=%fused_computation.104 | convolution fusion | flops 6576668672 | bytes 20250624 | tf_op jit(solution)/shard_map/dot_general | solution.py:31
  121.8 38.7 %convert_reduce_fusion = (f32[2048]{0:T(1024)}, bf16[1568,2048]{1,0:T(8,128)(2,1)S(1)}, f32[1568,2048]{1,0:T(8,128)}) fusion(f32[1568,2048]{1,0:T(8,128)S(1)} %fusion.23, f32[2048]{0:T(1024)S(1)} %copy-done.37, bf16[1568,1024]{1,0:T(8,128)(2,1)S(1)} %copy-done.8, bf16[2048,1024]{1,0:T(8,128)(2,1)S(1)} %copy-done.44), kind=kOutput, calls=%fused_computation.2 | convolution fusion | flops 6817511424 | bytes 39534592 | tf_op jit(solution)/shard_map/dot_general | solution.py:35
  160.6 2.7 copy-done.50
  163.3 8.4 %convolution_convert_fusion.2 = bf16[1568,1024]{1,0:T(8,128)(2,1)} fusion(bf16[1568,2048]{1,0:T(8,128)(2,1)S(1)} %get-tuple-element.64, bf16[1024,2048]{1,0:T(8,128)(2,1)S(1)} %copy-done.43), kind=kOutput, calls=%fused_computation.38 | convolution fusion | flops 6578274304 | bytes 13828096 | tf_op jit(solution)/shard_map/dot_general | solution.py:35
  171.8 0.4 reduce-scatter.7.cloned.1.call-start
  172.3 10.9 %multiply_convert_fusion = bf16[1568,2048]{1,0:T(8,128)(2,1)S(1)} fusion(f32[1568,2048]{1,0:T(8,128)} %get-tuple-element.65, f32[1568,2048]{1,0:T(8,128)} %copy-done.7, f32[2048]{0:T(1024)S(1)} %copy-done.37), kind=kLoop, calls=%fused_computation.4 | loop fusion | flops 12845056 | bytes 32120832 | tf_op jit(solution)/shard_map/convert_element_type | solution.py:420
  183.2 2.7 copy-done.12
  185.9 8.2 %convolution_convert_fusion.3 = bf16[1568,1024]{1,0:T(8,128)(2,1)} fusion(bf16[1568,2048]{1,0:T(8,128)(2,1)S(1)} %multiply_convert_fusion, bf16[2048,1024]{1,0:T(8,128)(2,1)S(1)} %copy-done.45), kind=kOutput, calls=%fused_computation.39 | convolution fusion | flops 6578274304 | bytes 13828096 | tf_op jit(solution)/shard_map/dot_general | solution.py:31
  194.2 5.4 convert_element_type.122
  199.7 4.6 fusion.12
  204.3 2.4 reduce-scatter.7.cloned.1.call-done
  206.7 5.1 fusion.21
  211.8 1.7 copy-done.3
  213.4 1.5 fusion.16
  215.2 12.8 %convolution_convert_fusion.refs_8_ = bf16[1024,2048]{1,0:T(8,128)(2,1)} fusion(bf16[1568,1024]{1,0:T(8,128)(2,1)} %all-gather.5.cloned.1.call-done, bf16[1568,2048]{1,0:T(8,128)(2,1)} %copy-done.50), kind=kOutput, calls=%fused_computation.36 | convolution fusion | flops 6578765824 | bytes 13828096 | tf_op jit(solution)/shard_map/dot_general | solution.py:39
  228.1 11.5 %convolution_convert_fusion.1.refs_7_ = bf16[2048,1024]{1,0:T(8,128)(2,1)} fusion(bf16[1568,2048]{1,0:T(8,128)(2,1)} %copy-done.12, bf16[1568,1024]{1,0:T(8,128)(2,1)S(1)} %copy-done.9), kind=kOutput, calls=%fused_computation.37 | convolution fusion | flops 6578765824 | bytes 13828096 | tf_op jit(solution)/shard_map/dot_general | solution.py:39
  239.5 4.9 convolution_convert_fusion.5.refs_3_
  244.5 93.8 %attend_back.1 = (bf16[1568,512]{1,0:T(8,128)(2,1)}, bf16[1568,512]{1,0:T(8,128)(2,1)}, bf16[1568,512]{1,0:T(8,128)(2,1)}, bf16[48,1024]{1,0:T(8,128)(2,1)}, bf1...) custom-call(bf16[1568,512]{1,0:T(8,128)(2,1)} %add_convert_fusion.7., ...), custom_call_target="tpu_custom_call" | custom-call | flops 40282095616 | bytes 39337984 | tf_op jit(solution)/shard_map/attend_back/pallas_call | solution.py:296
  338.3 3.8 fusion.14
  342.1 1.9 fusion.15
  344.0 3.8 add_convert_fusion.1
  347.9 0.7 all-gather.7.cloned.1.call-update
  348.7 2.7 convert_reduce_fusion.7
  351.5 4.5 convolution_convert_fusion.10.refs_6_
  356.0 3.1 convolution_convert_fusion.8.refs_8_
  359.2 3.7 multiply_reduce_fusion.1
  362.9 3.7 fusion.13
  366.6 5.5 add_convert_fusion.3
  372.2 1.9 convert_reduce_fusion.5
  374.3 2.7 convert_reduce_fusion.1
  377.1 4.7 convolution_convert_fusion.9.refs_7_
  381.8 3.1 convolution_convert_fusion.7.refs_9_
  384.9 3.4 psum.7
  388.4 0.6 pad_bitcast_fusion.refs_10_
  389.0 152.5 %spread_and_sum.1 = (bf16[2048,1024]{1,0:T(8,128)(2,1)}, bf16[1024,2048]{1,0:T(8,128)(2,1)}, bf16[1024,512]{1,0:T(8,128)(2,1)}, bf16[1024,512]{1,0:T(8,128)(2,1)...) custom-call(bf16[48,1024]{1,0:T(8,128)(2,1)} %get-tuple-element.42.refs_0_, ...), custom_call_target="tpu_custom_call" | custom-call | tf_op jit(solution)/shard_map/spread_and_sum/pallas_call | solution.py:361
  541.6 6.8 %convert_element_type.139 = f32[1024,2048]{1,0:T(8,128)} convert(bf16[1024,2048]{1,0:T(8,128)(2,1)} %get-tuple-element.53) | non-fusion elementwise | flops 2097152 | bytes 12582912 | tf_op jit(solution)/shard_map/convert_element_type | solution.py:482
  548.4 4.4 convert_element_type.140
  552.8 1.6 convert_element_type.138
  554.4 0.6 slice_bitcast_fusion.16
  555.0 0.6 slice_bitcast_fusion.9
  555.6 0.6 slice_bitcast_fusion.10
  556.2 3.2 convert_bitcast_fusion
  559.4 4.1 copy.40
  563.5 1.7 copy.41
  (129 shorter events, 1.5 us)
Async XLA Ops:
  7.2 64.3 %copy-start = (bf16[512,1024]{1,0:T(8,128)(2,1)S(1)}, bf16[512,1024]{1,0:T(8,128)(2,1)}, u32[]{:S(2)}) copy-start(bf16[512,1024]{1,0:T(8,128)(2,1)} %param.21) | copy-start | bytes 3145732
  7.2 4.0 copy-start.29
  7.2 4.0 copy-start.39
  7.2 83.4 %reduce-scatter.5.cloned.1.call-start = ((), (), s32[]{:S(2)}) async-start(), calls=%async_computation.4 | async-start | bytes 4816896 | tf_op jit(solution)/shard_map/reduce_scatter | solution.py:402
  7.3 3.0 copy-start.2
  11.3 1.9 copy-start.23
  12.8 6.5 %copy-start.14 = (bf16[1568,1024]{1,0:T(8,128)(2,1)}, bf16[1568,1024]{1,0:T(8,128)(2,1)S(1)}, u32[]{:S(2)}) copy-start(bf16[1568,1024]{1,0:T(8,128)(2,1)S(1)} %add_convert_fusion.2) | copy-start | bytes 9633796
  13.1 3.1 copy-start.46
  16.2 3.0 copy-start.47
  76.5 35.4 %all-gather.5.cloned.1.call-start = ((), (), s32[]{:S(2)}) async-start(), calls=%async_computation.5 | async-start | bytes 4816896 | tf_op jit(solution)/shard_map/all_gather | solution.py:405
  76.8 13.9 %copy-start.40 = (f32[1024]{0:T(1024)S(1)}, f32[1024]{0:T(1024)}, u32[]{:S(2)}) copy-start(f32[1024]{0:T(1024)} %param.22) | copy-start | bytes 12292
  94.3 1.6 copy-start.1
  94.3 2.2 copy-start.31
  94.3 2.2 copy-start.41
  94.3 1.6 copy-start.25
  94.8 0.6 copy-start.33
  95.9 0.6 copy-start.27
  98.3 23.5 %copy-start.37 = (f32[2048]{0:T(1024)S(1)}, f32[2048]{0:T(1024)}, u32[]{:S(2)}) copy-start(f32[2048]{0:T(1024)} %param.26) | copy-start | bytes 24580
  98.3 101.4 %reduce-scatter.9.cloned.1.call-start = ((), (), s32[]{:S(2)}) async-start(), calls=%async_computation.8 | async-start | bytes 4816896 | tf_op jit(solution)/shard_map/reduce_scatter | solution.py:402
  111.9 9.9 %copy-start.8 = (bf16[1568,1024]{1,0:T(8,128)(2,1)S(1)}, bf16[1568,1024]{1,0:T(8,128)(2,1)}, u32[]{:S(2)}) copy-start(bf16[1568,1024]{1,0:T(8,128)(2,1)} %param.29) | copy-start | bytes 9633796
  111.9 9.9 %copy-start.44 = (bf16[2048,1024]{1,0:T(8,128)(2,1)S(1)}, bf16[2048,1024]{1,0:T(8,128)(2,1)}, u32[]{:S(2)}) copy-start(bf16[2048,1024]{1,0:T(8,128)(2,1)} %param.27) | copy-start | bytes 12582916
  121.8 38.8 %copy-start.7 = (f32[1568,2048]{1,0:T(8,128)}, f32[1568,2048]{1,0:T(8,128)S(1)}, u32[]{:S(2)}) copy-start(f32[1568,2048]{1,0:T(8,128)S(1)} %fusion.23) | copy-start | bytes 38535172
  121.8 41.5 %copy-start.43 = (bf16[1024,2048]{1,0:T(8,128)(2,1)S(1)}, bf16[1024,2048]{1,0:T(8,128)(2,1)}, u32[]{:S(2)}) copy-start(bf16[1024,2048]{1,0:T(8,128)(2,1)} %param.25) | copy-start | bytes 12582916
  160.6 2.7 copy-start.50
  171.8 34.9 %reduce-scatter.7.cloned.1.call-start = ((), (), s32[]{:S(2)}) async-start(), calls=%async_computation.6 | async-start | bytes 4816896 | tf_op jit(solution)/shard_map/reduce_scatter | solution.py:402
  172.2 13.7 %copy-start.45 = (bf16[2048,1024]{1,0:T(8,128)(2,1)S(1)}, bf16[2048,1024]{1,0:T(8,128)(2,1)}, u32[]{:S(2)}) copy-start(bf16[2048,1024]{1,0:T(8,128)(2,1)} %param.27) | copy-start | bytes 12582916
  183.2 2.8 copy-start.12
  194.1 5.5 copy-start.26
  194.1 5.5 copy-start.28
  194.1 5.5 copy-start.32
  194.2 45.4 %all-gather.9.cloned.1.call-start = ((), (), s32[]{:S(2)}) async-start(), calls=%async_computation.9 | async-start | bytes 4816896 | tf_op jit(solution)/shard_map/all_gather | solution.py:405
  199.6 4.6 copy-start.34
  199.6 7.1 %copy-start.42 = (f32[1024]{0:T(1024)S(1)}, f32[1024]{0:T(1024)}, u32[]{:S(2)}) copy-start(f32[1024]{0:T(1024)} %param.28) | copy-start | bytes 12292
  199.7 7.0 %copy-start.11 = (bf16[784,1024]{1,0:T(8,128)(2,1)S(1)}, bf16[784,1024]{1,0:T(8,128)(2,1)}, u32[]{:S(2)}) copy-start(bf16[784,1024]{1,0:T(8,128)(2,1)} %reduce-scatter.9.cloned.1.call-done) | copy-start | bytes 4816900
  206.7 6.7 %copy-start.5 = (f32[1568,1024]{1,0:T(8,128)S(1)}, f32[1568,1024]{1,0:T(8,128)}, u32[]{:S(2)}) copy-start(f32[1568,1024]{1,0:T(8,128)} %convert_element_type.122) | copy-start | bytes 19267588
  211.8 1.7 copy-start.3
  215.0 144.2 %reduce-scatter.11.cloned.1.call-start = ((), (), s32[]{:S(2)}) async-start(), calls=%async_computation.10 | async-start | bytes 4816896 | tf_op jit(solution)/shard_map/reduce_scatter | solution.py:402
  215.2 12.9 %copy-start.9 = (bf16[1568,1024]{1,0:T(8,128)(2,1)S(1)}, bf16[1568,1024]{1,0:T(8,128)(2,1)}, u32[]{:S(2)}) copy-start(bf16[1568,1024]{1,0:T(8,128)(2,1)} %param.29) | copy-start | bytes 9633796
  338.3 3.8 copy-start.24
  338.3 3.8 copy-start.48
  342.1 1.9 copy-start.10
  347.9 3.5 copy-start.36
  347.9 26.4 %all-gather.7.cloned.1.call-start = ((), (), s32[]{:S(2)}) async-start(), calls=%async_computation.7 | async-start | bytes 4816896 | tf_op jit(solution)/shard_map/all_gather | solution.py:405
  348.6 210.8 %all-gather.11.cloned.1.call-start = ((), (), s32[]{:S(2)}) async-start(), calls=%async_computation.11 | async-start | bytes 4816896 | tf_op jit(solution)/shard_map/all_gather | solution.py:405
  348.7 2.9 copy-start.15
  356.0 3.1 copy-start.30
  359.2 3.7 copy-start.6
  362.8 3.8 copy-start.4
  374.3 2.9 copy-start.16
  377.1 4.7 copy-start.17
  377.1 4.7 copy-start.49
  381.8 6.6 %copy-start.38 = (f32[2048]{0:T(1024)S(1)}, f32[2048]{0:T(1024)}, u32[]{:S(2)}) copy-start(f32[2048]{0:T(1024)} %get-tuple-element.63) | copy-start | bytes 24580
  541.6 6.8 %copy-start.13 = (bf16[2048,1024]{1,0:T(8,128)(2,1)S(1)}, bf16[2048,1024]{1,0:T(8,128)(2,1)}, u32[]{:S(2)}) copy-start(bf16[2048,1024]{1,0:T(8,128)(2,1)} %get-tuple-element.54) | copy-start | bytes 12582916
  548.4 4.4 copy-start.22
  548.4 6.0 %copy-start.35 = (f32[128,128]{1,0:T(8,128)S(1)}, f32[128,128]{1,0:T(8,128)}, u32[]{:S(2)}) copy-start(f32[128,128]{1,0:T(8,128)} %get-tuple-element.48) | copy-start | bytes 196612
  552.8 3.4 copy-start.19
  552.8 3.4 copy-start.20
  552.8 3.4 copy-start.21
  559.4 4.1 copy-start.18
Sparse Core Ops, SparseCore 0:
  76.6 13.9 reduce-scatter.4
  98.4 13.4 all-gather.4
  171.9 12.4 reduce-scatter.8
  194.2 12.4 reduce-scatter.6
  215.1 13.4 all-gather.8
  348.0 11.1 reduce-scatter.10
  360.7 13.5 all-gather.6
  376.4 13.3 all-gather.10
